TPU v7x, 128 devices: a whole 4x4x4 slice. The times are simulated.
128 devices in a mesh: inst: 1, dev: 64 (over z, y, x), side: 2 (over core).
Axes of the slice: x: 4, y: 4, z: 4, core: 2. Of those that a mesh axis runs over, the one named last changes fastest.
Arguments:
- hidden: bfloat16 [512, 3072], P(('inst', 'dev'))
- cache_len: int32 [512], P(('inst', 'dev'))
- k_cache: bfloat16 [1, 512, 8, 256, 128], P(None, ('inst', 'dev'))
- v_cache: bfloat16 [1, 512, 8, 256, 128], P(None, ('inst', 'dev'))
- w_q: bfloat16 [1, 3072, 3072], replicated
- w_kv: bfloat16 [1, 3072, 2048], replicated
- w_o: bfloat16 [1, 3072, 3072], replicated
- attn_gain: float32 [1, 3072], replicated
- ffn_gain: float32 [1, 3072], replicated
- w_gate: bfloat16 [1, 3072, 8192], P(None, None, 'dev')
- w_up: bfloat16 [1, 3072, 8192], P(None, None, 'dev')
- w_down: bfloat16 [1, 8192, 3072], P(None, 'dev')
Outputs:
- output: bfloat16 [512, 3072], P(('inst', 'dev', 'side'))
All inputs are finite; a program needn't handle non-finite values.
Results may differ from a plain program's by a relative error of at most 0.0121802.
Values are sent between devices in bfloat16 or wider.
A program may use at most 1 GiB of HBM per device.

v0:
```python
import jax
import jax.numpy as jnp
from jax import lax
from jax.sharding import PartitionSpec as P

EPS = 1e-5
ROPE_BASE = 10000.0


def rms_norm(rows, gain):
    rows_f = rows.astype(jnp.float32)
    inv_rms = lax.rsqrt(jnp.mean(rows_f * rows_f, axis=-1, keepdims=True) + EPS)
    return (rows_f * inv_rms * gain).astype(jnp.bfloat16)


def rotary(vecs, positions):
    half_dim = vecs.shape[-1] // 2
    freqs = ROPE_BASE ** (-jnp.arange(half_dim, dtype=jnp.float32) / half_dim)
    angle = positions.astype(jnp.float32)[:, None, None] * freqs
    cos_part = jnp.cos(angle)
    sin_part = jnp.sin(angle)
    first = vecs[..., :half_dim]
    second = vecs[..., half_dim:]
    return jnp.concatenate([first * cos_part - second * sin_part, second * cos_part + first * sin_part], axis=-1)


def attention_layer(x_rows, lengths, k_seq, v_seq, q_weight, kv_weight, o_weight, gain_attn):
    count = x_rows.shape[0]
    kv_heads = k_seq.shape[1]
    head_dim = k_seq.shape[-1]
    normed = rms_norm(x_rows, gain_attn)
    q_all = jnp.dot(normed, q_weight, preferred_element_type=jnp.float32).reshape(count, -1, head_dim)
    kv_all = jnp.dot(normed, kv_weight, preferred_element_type=jnp.float32).reshape(count, 2, kv_heads, head_dim)
    q_rows = rotary(q_all, lengths).astype(jnp.bfloat16).reshape(count, kv_heads, -1, head_dim)
    k_new = rotary(kv_all[:, 0], lengths).astype(jnp.bfloat16)
    v_new = kv_all[:, 1].astype(jnp.bfloat16)
    scale = head_dim ** -0.5
    scores = jnp.einsum('nkgd,nksd->nkgs', q_rows, k_seq, preferred_element_type=jnp.float32) * scale
    valid = jnp.arange(k_seq.shape[2])[None, None, None, :] < lengths[:, None, None, None]
    scores = jnp.where(valid, scores, -1e30)
    self_score = jnp.einsum('nkgd,nkd->nkg', q_rows, k_new, preferred_element_type=jnp.float32) * scale
    row_max = jnp.maximum(jnp.max(scores, axis=-1), self_score)
    exp_scores = jnp.exp(scores - row_max[..., None])
    self_exp = jnp.exp(self_score - row_max)
    total_exp = jnp.sum(exp_scores, axis=-1) + self_exp
    mixed = jnp.einsum('nkgs,nksd->nkgd', exp_scores.astype(jnp.bfloat16), v_seq, preferred_element_type=jnp.float32)
    mixed = mixed + self_exp.astype(jnp.bfloat16).astype(jnp.float32)[..., None] * v_new.astype(jnp.float32)[:, :, None, :]
    mixed = (mixed / total_exp[..., None]).astype(jnp.bfloat16).reshape(count, -1)
    attn_out = jnp.dot(mixed, o_weight, preferred_element_type=jnp.float32)
    return (x_rows.astype(jnp.float32) + attn_out).astype(jnp.bfloat16)


def ffn_partial(h_rows, gate_weight, up_weight, down_weight):
    gate = jnp.dot(h_rows, gate_weight, preferred_element_type=jnp.float32)
    up_proj = jnp.dot(h_rows, up_weight, preferred_element_type=jnp.float32)
    act_rows = (jax.nn.silu(gate) * up_proj).astype(jnp.bfloat16)
    return jnp.dot(act_rows, down_weight, preferred_element_type=jnp.float32)


def pair_rows(local, slot, half_side):
    shaped = local.reshape((2, half_side, local.shape[0] // (2 * half_side)) + local.shape[1:])
    picked = lax.dynamic_index_in_dim(shaped, slot, axis=1, keepdims=False)
    return picked.reshape((-1,) + local.shape[1:])


def keep_rows(x_in):
    return x_in


def skip_ffn(h_in):
    return jnp.zeros(h_in.shape, jnp.float32)


def solution(mesh):
    n_side = mesh.shape['side']
    half_side = n_side // 2
    to_ffn = [(slot, slot + half_side) for slot in range(half_side)]
    to_attn = [(slot + half_side, slot) for slot in range(half_side)]
    batch_axes = ('inst', 'dev')
    in_specs = (
        P(batch_axes, None),
        P(batch_axes),
        P(None, batch_axes, None, None, None),
        P(None, batch_axes, None, None, None),
        P(), P(), P(), P(), P(),
        P(None, None, 'dev'),
        P(None, None, 'dev'),
        P(None, 'dev', None),
    )
    out_specs = P(('inst', 'dev', 'side'), None)

    def device_fn(hidden, cache_len, k_cache, v_cache, w_q, w_kv, w_o, attn_gain, ffn_gain, w_gate, w_up, w_down):
        side_idx = lax.axis_index('side')
        is_attn = side_idx < half_side
        slot = side_idx % half_side
        rows = hidden.shape[0] // n_side
        n_layers = w_q.shape[0]
        x_pair = pair_rows(hidden, slot, half_side)
        lengths = pair_rows(cache_len, slot, half_side)
        for layer in range(n_layers):
            def attn_branch(x_in, layer=layer):
                k_seq = pair_rows(k_cache[layer], slot, half_side)
                v_seq = pair_rows(v_cache[layer], slot, half_side)
                return attention_layer(x_in, lengths, k_seq, v_seq, w_q[layer], w_kv[layer], w_o[layer], attn_gain[layer])

            def ffn_branch(h_in, layer=layer):
                return ffn_partial(h_in, w_gate[layer], w_up[layer], w_down[layer])

            x_pair = lax.cond(is_attn, attn_branch, keep_rows, x_pair)
            sent = lax.ppermute(x_pair, 'side', to_ffn)
            h_rows = rms_norm(sent, ffn_gain[layer])
            h_all = lax.all_gather(h_rows, 'dev', axis=0, tiled=True)
            part_sum = lax.cond(is_attn, skip_ffn, ffn_branch, h_all)
            summed = lax.psum_scatter(part_sum, 'dev', scatter_dimension=0, tiled=True)
            x_ffn = (sent.astype(jnp.float32) + summed.astype(jnp.bfloat16).astype(jnp.float32)).astype(jnp.bfloat16)
            if layer + 1 < n_layers:
                x_pair = lax.ppermute(x_ffn, 'side', to_attn)
            else:
                back = lax.ppermute(x_ffn[:rows], 'side', to_attn)
                out_rows = jnp.where(is_attn, back, x_ffn[rows:])
        return out_rows

    return jax.shard_map(device_fn, mesh=mesh, in_specs=in_specs, out_specs=out_specs, check_vma=False)
```

profile of v0, /device:TPU:1, one launch (start us, length us, event | category | flops | bytes accessed | tf_op | source)
XLA Modules:
  0.0 394.9 jit_solution(11086734957369061893)
XLA Ops:
  6.5 0.0 copy-start.2
  6.5 0.0 all-gather.2.cloned.1.call-start
  6.5 0.8 copy-done.2
  7.3 0.0 copy-start.4
  7.3 1.4 collective-permute-start
  8.8 71.2 %collective-permute-done = bf16[8,3072]{1,0:T(8,128)(2,1)S(1)} collective-permute-done((bf16[8,3072]{1,0:T(8,128)(2,1)S(1)}, bf16[8,3072]{1,0:T(8,128)(2,1)S(1)}, u32[]{:S(2)}, u32[]{:S(2)}) %collective-permute-start) | collective-permute-done | bytes 49184 | tf_op jit(solution)/shard_map/ppermute | solution.py:110
  79.9 0.1 fusion.59
  80.1 0.0 copy-done.4
  80.1 0.7 fusion.61
  80.8 0.0 all-gather.2.cloned.1.call-update
  80.8 0.0 reduce-scatter.2.cloned.1.call-start
  80.9 67.4 %all-gather.2.cloned.1.call-done = bf16[512,3072]{1,0:T(8,128)(2,1)} async-done(((bf16[8,3072]{1,0:T(8,128)(2,1)}), bf16[512,3072]{1,0:T(8,128)(2,1)}) %all-gather.2.cloned.1.call-update) | async-done | bytes 3145744 | tf_op jit(solution)/shard_map/all_gather | solution.py:112
  148.3 10.6 %conditional.3 = (f32[512,3072]{1,0:T(8,128)}) conditional(s32[]{:T(128)} %convert_element_type.80, (bf16[1,3072,128]{2,1,0:T(8,128)(2,1)}, bf16[512,3072]{1,0:T(8,128)(2,1)}, bf16[1,3072,128]{2,1,0:T(8,128)(2,1)}, bf16[1,128,3072]{2,1,0:T(8,128)(2,1)}) %tuple.20, () %tuple.21), branch_computations={%region_6.7_spmd, %region_7.8_spmd} | conditional | flops 1208352768 | bytes 28049444 | solution.py:113
  148.3 0.0 copy-start
  148.3 3.2 fusion.50
  151.5 0.0 copy-done
  151.5 7.4 %fusion.46 = f32[512,3072]{1,0:T(8,128)} fusion(bf16[512,3072]{1,0:T(8,128)(2,1)S(1)} %copy-done, bf16[1,128,3072]{2,1,0:T(8,128)(2,1)} %get-tuple-element.88, bf16[1,3072,128]{2,1,0:T(8,128)(2,1)} %get-tuple-element.87, f32[512,128]{1,0:T(8,128)S(1)} %fusion.50), kind=kOutput, calls=%fused_computation.49 | convolution fusion | flops 805699584 | bytes 11272192 | tf_op jit(solution)/shard_map/cond/branch_0_fun/dot_general | solution.py:57
  158.9 0.0 reduce-scatter.2.cloned.1.call-update
  158.9 222.1 %reduce-scatter.2.cloned.1.call-done = f32[8,3072]{1,0:T(8,128)} async-done(((f32[512,3072]{1,0:T(8,128)}), f32[8,3072]{1,0:T(8,128)}) %reduce-scatter.2.cloned.1.call-update) | async-done | bytes 98320 | tf_op jit(solution)/shard_map/reduce_scatter | solution.py:114
  381.1 0.9 fusion.62
  382.0 4.6 %collective-permute-start.1 = (bf16[4,3072]{1,0:T(4,128)(2,1)S(1)}, bf16[4,3072]{1,0:T(4,128)(2,1)S(1)}, u32[]{:S(2)}, u32[]{:S(2)}) collective-permute-start(bf16[4,3072]{1,0:T(4,128)(2,1)S(1)} %slice.39), channel_id=1, source_target_pairs={{1,0},{3,2},{5,4},{7,6},{9,8},{11,10},{13,12},{15,14},{17,16},{19,... | collective-permute-start | bytes 73736 | tf_op jit(solution)/shard_map/ppermute | solution.py:119
  386.6 0.8 collective-permute-done.1
  387.4 0.6 slice_select_fusion
  (3 shorter events, 0.0 us)
Async XLA Ops:
  6.5 0.8 copy-start.2
  6.5 141.7 %all-gather.2.cloned.1.call-start = ((), (), s32[]{:S(2)}) async-start(), calls=%async_computation.1 | async-start | bytes 3194880 | tf_op jit(solution)/shard_map/all_gather | solution.py:112
  7.3 72.8 %copy-start.4 = (f32[1,3072]{1,0:T(1,128)S(1)}, f32[1,3072]{1,0:T(1,128)}, u32[]{:S(2)}) copy-start(f32[1,3072]{1,0:T(1,128)} %param.24) | copy-start | bytes 36868
  7.3 72.6 %collective-permute-start = (bf16[8,3072]{1,0:T(8,128)(2,1)S(1)}, bf16[8,3072]{1,0:T(8,128)(2,1)S(1)}, u32[]{:S(2)}, u32[]{:S(2)}) collective-permute-start(bf16[8,3072]{1,0:T(8,128)(2,1)S(1)} %get-tuple-element.117), channel_id=1, source_target_pairs={{0,1},{2,3},{4,5},{6,7},{8,9},{10,11},{12,13},{14,15},{16,17},{18,... | collective-permute-start | bytes 147464 | tf_op jit(solution)/shard_map/ppermute | solution.py:110
  80.8 300.3 %reduce-scatter.2.cloned.1.call-start = ((), (), s32[]{:S(2)}) async-start(), calls=%async_computation.2 | async-start | bytes 6389760 | tf_op jit(solution)/shard_map/reduce_scatter | solution.py:114
  148.3 3.2 copy-start
  382.0 5.4 %collective-permute-start.1 = (bf16[4,3072]{1,0:T(4,128)(2,1)S(1)}, bf16[4,3072]{1,0:T(4,128)(2,1)S(1)}, u32[]{:S(2)}, u32[]{:S(2)}) collective-permute-start(bf16[4,3072]{1,0:T(4,128)(2,1)S(1)} %slice.39), channel_id=1, source_target_pairs={{1,0},{3,2},{5,4},{7,6},{9,8},{11,10},{13,12},{15,14},{17,16},{19,... | collective-permute-start | bytes 73736 | tf_op jit(solution)/shard_map/ppermute | solution.py:119
Sparse Core Ops, SparseCore 0:
  80.9 67.2 all-gather.1
  159.1 221.9 reduce-scatter.1
where the time goes:
time: 396 us; the launch traced here: 395 us
  waiting for transfers between devices  362 us (91%)
  between operations  13.4 us (3%)
  matrix products  10.6 us (3%)
  starting transfers between devices  6.02 us (2%)
    reduce_scatter x1, waiting for transfers between devices, device_fn(): summed = lax.psum_scatter(part_sum, 'dev', scatter_dimension=0, tiled=True)  222 us
    ppermute x1, waiting for transfers between devices, device_fn(): sent = lax.ppermute(x_pair, 'side', to_ffn)  71.2 us
    all_gather x1, waiting for transfers between devices, device_fn(): h_all = lax.all_gather(h_rows, 'dev', axis=0, tiled=True)  67.4 us
  transfers between devices with their start and end apart: 4, of which 4 were waited for; matrix products, arithmetic and copies ran while one was open for 0% of the time, Pallas kernels for 0%

commit v1 on v0

v1 whole, which is shorter than its diff:
```python
import numpy as np
import jax
import jax.numpy as jnp
from jax import lax
from jax.experimental import pallas as pl
from jax.experimental.pallas import tpu as pltpu
from jax.sharding import PartitionSpec as P

EPS = 1e-5
ROPE_BASE = 10000.0
MESH = pl.DeviceIdType.MESH
F32 = jnp.float32
BF16 = jnp.bfloat16

N_DEV = 64
D = 3072
DH = D // 2
PART = 512
FFC = 128
SEQ = 256
HEAD = 128
KVH = 4
GROUP = 3
GRP = 8
NC = D // GRP
ROWS = 256


def coords(dev):
    return dev % 4, (dev // 4) % 4, dev // 16


def flat(x, y, z):
    return z * 16 + y * 4 + x


def ring_slot(part, dev):
    x, y, z = coords(dev)
    if part == 0:
        return x, z * 4 + y
    if part == 1:
        return y, z * 4 + x
    return z, y * 4 + x


def chip_at(part, ring, plane):
    if part == 0:
        return flat(ring, plane % 4, plane // 4)
    if part == 1:
        return flat(plane % 4, ring, plane // 4)
    return flat(plane % 4, plane // 4, ring)


def body(lens, hid, again, fgain, freq, kc, vc, wq, wkv, wo, wg, wu, wd, out,
         wq_b, wkv_b, wo_b, kc_b, vc_b, wgu_b, wd_b, a_b, kv_b, o_b, p_own, p_oth, x1f,
         hbuf, h2, gu_o, gu_m, gu_r, ubuf, y2, ysend, yrecv, tab, lens_v,
         w_sem, kv_sem, c_sem, wo_sem, f_sem, wd_sem, wds_sem, wdr_sem,
         ps_sem, pr_sem, a1s, a1r, a2s, a2r, gs_sem, gr_sem, us_sem, ur_sem, ys_sem, yr_sem):
    dev = lax.axis_index("dev")
    side = lax.axis_index("side")
    me = dev * 2 + side
    cx, cy, cz = coords(dev)
    j_me = (cx % 2) + 2 * (cy % 2) + 4 * (cz % 2)
    other = 1 - side

    def kv_copy(i):
        col = pl.multiple_of(i * 1024 + side * 512, 128)
        return pltpu.make_async_copy(wkv.at[0, :, pl.ds(col, 512)], wkv_b.at[i], kv_sem.at[i])

    def q_copy(h):
        col = pl.multiple_of(side * DH + h * 384, 128)
        return pltpu.make_async_copy(wq.at[0, :, pl.ds(col, 384)], wq_b.at[h], w_sem.at[h])

    def c_copy(i):
        src, dst = (kc, kc_b) if i == 0 else (vc, vc_b)
        return pltpu.make_async_copy(src.at[0, :, pl.ds(side * KVH, KVH)], dst, c_sem.at[i])

    def o_copy(n):
        row = pl.multiple_of(side * DH, 128)
        return pltpu.make_async_copy(wo.at[0, pl.ds(row, DH), pl.ds(pl.multiple_of(n * 512, 128), 512)], wo_b.at[n], wo_sem.at[n])

    def f_copy(i):
        row = pl.multiple_of(side * DH, 128)
        src = wg if i == 0 else wu
        return pltpu.make_async_copy(src.at[0, pl.ds(row, DH), :], wgu_b.at[:, pl.ds(i * FFC, FFC)], f_sem.at[i])

    wd_own = pltpu.make_async_copy(wd.at[0, :, pl.ds(pl.multiple_of(j_me * NC, 128), NC)], wd_b.at[j_me], wd_sem)

    kv_copy(0).start()
    kv_copy(1).start()
    q_copy(0).start()
    c_copy(0).start()
    c_copy(1).start()
    for h in range(1, KVH):
        q_copy(h).start()
    for n in range(6):
        o_copy(n).start()
    f_copy(0).start()
    f_copy(1).start()
    wd_own.start()

    barrier = pltpu.get_barrier_semaphore()

    def greet(i, c):
        t = (me + i) % (2 * N_DEV)
        pl.semaphore_signal(barrier, inc=1, device_id=(0, t // 2, t % 2), device_id_type=MESH)
        return c

    lax.fori_loop(1, 2 * N_DEV, greet, 0)

    rowb = lax.broadcasted_iota(jnp.int32, (8, 128), 0)
    lv = jnp.zeros((8, 128), jnp.int32)
    for b in range(8):
        lv = jnp.where(rowb == b, lens[b], lv)
    angle = lv.astype(F32) * freq[...]
    lane = lax.broadcasted_iota(jnp.int32, (8, 128), 1)
    sin = jnp.sin(angle)
    tab[0] = jnp.cos(angle)
    tab[1] = jnp.where(lane < 64, -sin, sin)
    lens_v[...] = jnp.concatenate([lv, lv, lv], axis=0)

    def rotary(v):
        return v * tab[0] + pltpu.roll(v, 64, axis=1) * tab[1]

    xf = hid[...].astype(F32)
    inv = lax.rsqrt(jnp.mean(xf * xf, axis=-1, keepdims=True) + EPS)
    a_b[...] = (xf * inv * again[...]).astype(BF16)

    for i in range(2):
        kv_copy(i).wait()
        kv = jnp.dot(a_b[...], wkv_b[i], preferred_element_type=F32)
        for h in range(KVH):
            v = kv[:, h * HEAD:(h + 1) * HEAD]
            if i == 0:
                v = rotary(v)
            kv_b[i, h] = v.astype(BF16).astype(F32)

    pl.semaphore_wait(barrier, 2 * N_DEV - 1)

    def block_peer(k):
        px = cx + (k % 2) * (1 - 2 * (cx % 2))
        py = cy + ((k // 2) % 2) * (1 - 2 * (cy % 2))
        pz = cz + (k // 4) * (1 - 2 * (cz % 2))
        return flat(px, py, pz), (px % 2) + 2 * (py % 2) + 4 * (pz % 2)

    def wd_copy(k):
        peer, j = block_peer(k)
        return pltpu.make_async_remote_copy(
            src_ref=wd.at[0, :, pl.ds(pl.multiple_of(j * NC, 128), NC)], dst_ref=wd_b.at[j_me],
            send_sem=wds_sem.at[k], recv_sem=wdr_sem.at[k], device_id=(0, peer, side), device_id_type=MESH)

    for k in range(1, GRP):
        wd_copy(k).start()

    rowm = lax.broadcasted_iota(jnp.int32, (24, SEQ), 0) % 8
    rowv = lax.broadcasted_iota(jnp.int32, (24, HEAD), 0) % 8
    pos = lax.broadcasted_iota(jnp.int32, (24, SEQ), 1)
    scale = HEAD ** -0.5
    c_copy(0).wait()
    c_copy(1).wait()

    def attend(h, c):
        q_copy(h).wait()
        q = jnp.dot(a_b[...], wq_b[h], preferred_element_type=F32)
        qf = jnp.concatenate([rotary(q[:, g * HEAD:(g + 1) * HEAD]) for g in range(GROUP)], axis=0)
        qb = qf.astype(BF16)
        k_new = kv_b[0, h]
        v_new = kv_b[1, h]
        k3 = jnp.concatenate([k_new, k_new, k_new], axis=0)
        v3 = jnp.concatenate([v_new, v_new, v_new], axis=0)
        self_score = jnp.sum(qb.astype(F32) * k3, axis=-1, keepdims=True) * scale
        s = jnp.zeros((24, SEQ), F32)
        for b in range(8):
            sb = lax.dot_general(qb, kc_b[b, h], (((1,), (1,)), ((), ())), preferred_element_type=F32)
            s = jnp.where(rowm == b, sb, s)
        limit = lens_v[...]
        limit = jnp.concatenate([limit, limit], axis=1)
        s = jnp.where(pos < limit, s * scale, -1e30)
        top = jnp.maximum(jnp.max(s, axis=-1, keepdims=True), self_score)
        e = jnp.exp(s - top)
        es = jnp.exp(self_score - top)
        total = jnp.sum(e, axis=-1, keepdims=True) + es
        eb = e.astype(BF16)
        m = jnp.zeros((24, HEAD), F32)
        for b in range(8):
            mb = jnp.dot(eb, vc_b[b, h], preferred_element_type=F32)
            m = jnp.where(rowv == b, mb, m)
        m = m + es.astype(BF16).astype(F32) * v3
        o = m / total
        for g in range(GROUP):
            o_b[h, :, g * HEAD:(g + 1) * HEAD] = o[g * 8:(g + 1) * 8].astype(BF16)
        return c

    lax.fori_loop(0, KVH, attend, 0)

    def p_copy(n):
        return pltpu.make_async_remote_copy(
            src_ref=p_own.at[n], dst_ref=p_oth.at[n], send_sem=ps_sem.at[n], recv_sem=pr_sem.at[n],
            device_id=(0, dev, other), device_id_type=MESH)

    o_all = jnp.concatenate([o_b[h] for h in range(KVH)], axis=1)

    def project(n, c):
        o_copy(n).wait()
        p_own[n] = jnp.dot(o_all, wo_b[n], preferred_element_type=F32)
        p_copy(n).start()
        return c

    lax.fori_loop(0, 6, project, 0)

    ssq = jnp.zeros((8, 1), F32)
    for n in range(6):
        p_copy(n).wait_recv()
        v = hid[:, n * 512:(n + 1) * 512].astype(F32) + (p_own[n] + p_oth[n])
        v = v.astype(BF16).astype(F32)
        x1f[n] = v
        ssq = ssq + jnp.sum(v * v, axis=-1, keepdims=True)
    inv1 = lax.rsqrt(ssq / D + EPS)

    for q in range(3):
        ring, plane = ring_slot(q, dev)
        v = x1f[side * 3 + q] * inv1 * fgain[side * 3 + q]
        hbuf[q, ring, plane] = v.astype(BF16)

    def a1_copy(q, k):
        ring, plane = ring_slot(q, dev)
        to = ((plane // 4 + k // 4) % 4) * 4 + (plane + k) % 4
        return pltpu.make_async_remote_copy(
            src_ref=hbuf.at[q, ring, plane], dst_ref=hbuf.at[q, ring, plane],
            send_sem=a1s.at[q], recv_sem=a1r.at[q],
            device_id=(0, chip_at(q, ring, to), side), device_id_type=MESH)

    def to_plane(k, c):
        for q in range(3):
            ring, plane = ring_slot(q, dev)
            to = ((plane // 4 + k // 4) % 4) * 4 + (plane % 4 + k % 4) % 4
            pltpu.make_async_remote_copy(
                src_ref=hbuf.at[q, ring, plane], dst_ref=hbuf.at[q, ring, plane],
                send_sem=a1s.at[q], recv_sem=a1r.at[q],
                device_id=(0, chip_at(q, ring, to), side), device_id_type=MESH).start()
        return c

    lax.fori_loop(1, 16, to_plane, 0)

    def a2_copy(q, k):
        ring, plane = ring_slot(q, dev)
        to = (ring + k) % 4
        return pltpu.make_async_remote_copy(
            src_ref=hbuf.at[q, ring], dst_ref=hbuf.at[q, ring],
            send_sem=a2s.at[q], recv_sem=a2r.at[q],
            device_id=(0, chip_at(q, to, plane), side), device_id_type=MESH)

    for q in range(3):
        pltpu.make_async_copy(hbuf.at[q, 0, pl.ds(0, 15)], hbuf.at[q, 0, pl.ds(0, 15)], a1r.at[q]).wait()
        for k in (1, 3, 2):
            a2_copy(q, k).start()
    for q in range(3):
        pltpu.make_async_copy(hbuf.at[q, pl.ds(0, 3)], hbuf.at[q, pl.ds(0, 3)], a2r.at[q]).wait()

    f_copy(0).wait()
    f_copy(1).wait()

    def arrange(half):
        def pair(i, c):
            for q in range(3):
                vs = []
                for t in range(2):
                    ring, plane = ring_slot(q, half * 32 + 2 * i + t)
                    vs.append(hbuf[q, ring, plane].astype(F32))
                h2[pl.ds(pl.multiple_of(i * 16, 16), 16), q * PART:(q + 1) * PART] = jnp.concatenate(vs, axis=0).astype(BF16)
            return c
        lax.fori_loop(0, 16, pair, 0)

    g_copy = pltpu.make_async_remote_copy(
        src_ref=gu_o, dst_ref=gu_r, send_sem=gs_sem, recv_sem=gr_sem, device_id=(0, dev, other), device_id_type=MESH)
    arrange(other)
    gu_o[...] = jnp.dot(h2[...], wgu_b[...], preferred_element_type=F32)
    g_copy.start()
    arrange(side)
    gu_m[...] = jnp.dot(h2[...], wgu_b[...], preferred_element_type=F32)
    g_copy.wait_recv()
    gate = gu_m[:, :FFC] + gu_r[:, :FFC]
    up = gu_m[:, FFC:] + gu_r[:, FFC:]
    ubuf[j_me] = (gate * jax.nn.sigmoid(gate) * up).astype(BF16)

    def u_copy(k):
        peer, _ = block_peer(k)
        return pltpu.make_async_remote_copy(
            src_ref=ubuf.at[j_me], dst_ref=ubuf.at[j_me], send_sem=us_sem.at[k], recv_sem=ur_sem.at[k],
            device_id=(0, peer, side), device_id_type=MESH)

    for k in range(1, GRP):
        u_copy(k).start()
    wd_own.wait()
    for k in range(1, GRP):
        wd_copy(k).wait_recv()
    for k in range(1, GRP):
        u_copy(k).wait_recv()
    u_all = jnp.concatenate([ubuf[j] for j in range(GRP)], axis=1)
    y2[...] = jnp.dot(u_all, wd_b[...].reshape(GRP * FFC, NC), preferred_element_type=F32)

    def cut(i, c):
        v = y2[pl.ds(pl.multiple_of(i * 8, 8), 8), :]
        ysend[2 * i] = v[0:4]
        ysend[2 * i + 1] = v[4:8]
        return c

    lax.fori_loop(0, 32, cut, 0)
    here = side == dev // 32

    def give(i, c):
        k = (i + me) % 64
        d = side * 32 + k // 2
        t = k % 2

        @pl.when(jnp.logical_or(d != dev, t != side))
        def _():
            pltpu.make_async_remote_copy(
                src_ref=ysend.at[k], dst_ref=yrecv.at[dev], send_sem=ys_sem, recv_sem=yr_sem,
                device_id=(0, d, t), device_id_type=MESH).start()
        return c

    lax.fori_loop(0, 64, give, 0)

    @pl.when(here)
    def _():
        yrecv[dev] = ysend[(dev % 32) * 2 + side]

    def wait_blocks(ref, sem):
        @pl.when(here)
        def _():
            pltpu.make_async_copy(ref.at[pl.ds(0, 63)], ref.at[pl.ds(0, 63)], sem).wait()

        @pl.when(jnp.logical_not(here))
        def _():
            pltpu.make_async_copy(ref, ref, sem).wait()

    wait_blocks(yrecv, yr_sem)
    x1 = jnp.concatenate([x1f[n] for n in range(6)], axis=1)
    x1 = jnp.where(side == 0, x1[0:4], x1[4:8])
    for j in range(GRP):
        acc = None
        for c in range(N_DEV):
            x, y, z = c % 4, (c // 4) % 4, c // 16
            if (x % 2) + 2 * (y % 2) + 4 * (z % 2) == j:
                acc = yrecv[c] if acc is None else acc + yrecv[c]
        out[:, j * NC:(j + 1) * NC] = (x1[:, j * NC:(j + 1) * NC] + acc.astype(BF16).astype(F32)).astype(BF16)

    for k in range(1, GRP):
        wd_copy(k).wait_send()
        u_copy(k).wait_send()
    for n in range(6):
        p_copy(n).wait_send()
    for q in range(3):
        pltpu.make_async_copy(hbuf.at[q, 0, pl.ds(0, 15)], hbuf.at[q, 0, pl.ds(0, 15)], a1s.at[q]).wait()
        pltpu.make_async_copy(hbuf.at[q, pl.ds(0, 3)], hbuf.at[q, pl.ds(0, 3)], a2s.at[q]).wait()
    g_copy.wait_send()
    wait_blocks(ysend, ys_sem)


def solution(mesh):
    batch_axes = ('inst', 'dev')
    in_specs = (
        P(batch_axes, None),
        P(batch_axes),
        P(None, batch_axes, None, None, None),
        P(None, batch_axes, None, None, None),
        P(), P(), P(), P(), P(),
        P(None, None, 'dev'),
        P(None, None, 'dev'),
        P(None, 'dev', None),
    )
    out_specs = P(('inst', 'dev', 'side'), None)
    half = HEAD // 2
    freqs = (ROPE_BASE ** (-np.arange(half, dtype=np.float64) / half)).astype(np.float32)
    freqs = np.concatenate([freqs, freqs])[None]

    def device_fn(hidden, cache_len, k_cache, v_cache, w_q, w_kv, w_o, attn_gain, ffn_gain, w_gate, w_up, w_down):
        vmem = pl.BlockSpec(memory_space=pltpu.VMEM)
        hbm = pl.BlockSpec(memory_space=pl.ANY)
        dma = pltpu.SemaphoreType.DMA
        return pl.pallas_call(
            body,
            out_shape=jax.ShapeDtypeStruct((4, D), BF16),
            in_specs=[pl.BlockSpec(memory_space=pltpu.SMEM)] + [vmem] * 4 + [hbm] * 8,
            out_specs=vmem,
            scratch_shapes=[
                pltpu.VMEM((KVH, D, 384), BF16),
                pltpu.VMEM((2, D, 512), BF16),
                pltpu.VMEM((6, DH, 512), BF16),
                pltpu.VMEM((8, KVH, SEQ, HEAD), BF16),
                pltpu.VMEM((8, KVH, SEQ, HEAD), BF16),
                pltpu.VMEM((DH, 2 * FFC), BF16),
                pltpu.VMEM((GRP, FFC, NC), BF16),
                pltpu.VMEM((8, D), BF16),
                pltpu.VMEM((2, KVH, 8, HEAD), F32),
                pltpu.VMEM((KVH, 8, 384), BF16),
                pltpu.VMEM((6, 8, 512), F32),
                pltpu.VMEM((6, 8, 512), F32),
                pltpu.VMEM((6, 8, 512), F32),
                pltpu.VMEM((3, 4, 16, 8, PART), BF16),
                pltpu.VMEM((ROWS, DH), BF16),
                pltpu.VMEM((ROWS, 2 * FFC), F32),
                pltpu.VMEM((ROWS, 2 * FFC), F32),
                pltpu.VMEM((ROWS, 2 * FFC), F32),
                pltpu.VMEM((GRP, ROWS, FFC), BF16),
                pltpu.VMEM((ROWS, NC), F32),
                pltpu.VMEM((64, 4, NC), F32),
                pltpu.VMEM((64, 4, NC), F32),
                pltpu.VMEM((2, 8, 128), F32),
                pltpu.VMEM((24, 128), jnp.int32),
                dma((KVH,)), dma((2,)), dma((2,)), dma((6,)), dma((2,)), dma, dma((GRP,)), dma((GRP,)),
                dma((6,)), dma((6,)), dma((3,)), dma((3,)), dma((3,)), dma((3,)), dma, dma,
                dma((GRP,)), dma((GRP,)), dma, dma,
            ],
            compiler_params=pltpu.CompilerParams(
                collective_id=0, has_side_effects=True, vmem_limit_bytes=60 * 1024 * 1024),
            name="decode_layer",
        )(cache_len, hidden, attn_gain, ffn_gain.reshape(6, 1, 512), jnp.asarray(freqs),
          k_cache, v_cache, w_q, w_kv, w_o, w_gate, w_up, w_down)

    return jax.shard_map(device_fn, mesh=mesh, in_specs=in_specs, out_specs=out_specs, check_vma=False)
```

time: 396 us -> 61.9 us (0.16)
  waiting for transfers between devices: 362 us -> 0 us
  Pallas kernels: 0 us -> 60.3 us
  between operations: 13.4 us -> 0.01 us
  matrix products: 10.6 us -> 0 us
  starting transfers between devices: 6.02 us -> 0 us
    reduce_scatter x1 -> x0, waiting for transfers between devices: 222 us -> none  [device_fn(): summed = lax.psum_scatter(part_sum, 'dev', scatter_dimension=0, tiled=True)]
    ppermute x2 -> x0, waiting for transfers between devices: 72 us -> none  [the longest x1 71.2 us: device_fn(): sent = lax.ppermute(x_pair, 'side', to_ffn)]
    all_gather x1 -> x0, waiting for transfers between devices: 67.4 us -> none  [device_fn(): h_all = lax.all_gather(h_rows, 'dev', axis=0, tiled=True)]
    pallas_call x0 -> x1, Pallas kernels: none -> 60.3 us  [device_fn(): pl.pallas_call(body, out_shape=jax.ShapeDtypeStruct((4, D), BF16), in_spe...]
    dot_general x2 -> x0, matrix products: 10.6 us -> none  [the longest x1 7.43 us: ffn_partial(): return jnp.dot(act_rows, down_weight, preferred_element_type=jnp.float32)]
    ppermute x2 -> x0, starting transfers between devices: 5.97 us -> none  [the longest x1 4.56 us: device_fn(): back = lax.ppermute(x_ffn[:rows], 'side', to_attn)]
  transfers between devices with their start and end apart: 4 -> 0, of which waited for: 4 -> 0; matrix products, arithmetic and copies ran while one was open for 0% -> 0% of each run, Pallas kernels for 0% -> 0%
where the time goes in v1:
time: 61.9 us; the launch traced here: 61.6 us
  Pallas kernels  60.3 us (97%)
  local copies, waits for them, and re-layouts  1.36 us (2%)
    pallas_call x1, Pallas kernels, device_fn(): pl.pallas_call(body, out_shape=jax.ShapeDtypeStruct((4, D), BF16), in_spe...  60.3 us
    unnamed x1, local copies, waits for them, and re-layouts  1.36 us

profile of v1, /device:TPU:1, one launch (start us, length us, event | category | flops | bytes accessed | tf_op | source)
XLA Modules:
  0.0 61.6 jit_solution(8409843323478677410)
XLA Ops:
  0.0 60.3 %decode_layer.1 = bf16[4,3072]{1,0:T(4,128)(2,1)} custom-call(s32[8]{0:T(128)} %lens.1, bf16[8,3072]{1,0:T(8,128)(2,1)} %hid.1, f32[1,3072]{1,0:T(1,128)} %again.1, f32[6,1,512]{2,1,0:T(1,128)} %bitcast.1, f32[1,128]{1,0:T(1,128)} %constant.2.clone.freq, bf16[1,8,8,256,128]{4,3,2,1,0:T(8,128)(2,1)} %kc.1, bf16[1,8,8,256,128]{4,3,2,1,0:T(8,128)(2,1)} %vc.1, ...), custom_call_target="tpu_custom_call" | custom-call | tf_op jit(solution)/shard_map/decode_layer/pallas_call | solution.py:382
  60.3 1.4 %copy.15 = bf16[4,3072]{1,0:T(4,128)(2,1)} copy(bf16[4,3072]{1,0:T(4,128)(2,1)} %decode_layer.1) | data formatting | bytes 49152

commit v2 on v0

v2 whole, which is shorter than its diff:
```python
import numpy as np
import jax
import jax.numpy as jnp
from jax import lax
from jax.experimental import pallas as pl
from jax.experimental.pallas import tpu as pltpu
from jax.sharding import PartitionSpec as P

EPS = 1e-5
ROPE_BASE = 10000.0
MESH = pl.DeviceIdType.MESH
F32 = jnp.float32
BF16 = jnp.bfloat16

N_DEV = 64
D = 3072
DH = D // 2
PART = 512
FFC = 128
SEQ = 256
HEAD = 128
KVH = 4
GROUP = 3
GRP = 8
NC = D // GRP
ROWS = 256
CHUNKS = 4
CH = ROWS // CHUNKS
KVC = 768
ORDER = (0, 1, 3, 2)


def coords(dev):
    return dev % 4, (dev // 4) % 4, dev // 16


def flat(x, y, z):
    return z * 16 + y * 4 + x


def ring_slot(part, dev):
    x, y, z = coords(dev)
    if part == 0:
        return x, z * 4 + y
    if part == 1:
        return y, z * 4 + x
    return z, y * 4 + x


def chip_at(part, ring, plane):
    if part == 0:
        return flat(ring, plane % 4, plane // 4)
    if part == 1:
        return flat(plane % 4, ring, plane // 4)
    return flat(plane % 4, plane // 4, ring)


def body(lens, hid_h, again_h, fgain_h, freq_h, kc, vc, wq, wkv, wo, wg, wu, wd, out,
         hid, again, fgain, freq,
         wq_b, wkv_b, wo_b, kc_b, vc_b, wgu_b, wd_b, a_b, kv_b, o_b, p_own, p_oth, x1f,
         hbuf, h2, gu_o, gu_m, gu_r, ubuf, ysend, yrecv, tab, lens_v,
         i_sem, w_sem, kv_sem, c_sem, wo_sem, f_sem, wd_sem, wds_sem, wdr_sem,
         ps_sem, pr_sem, a1s, a1r, a2s, a2r, a2f, gs_sem, gr_sem, us_sem, ur_sem, ys_sem, yr_sem):
    dev = lax.axis_index("dev")
    side = lax.axis_index("side")
    me = dev * 2 + side
    cx, cy, cz = coords(dev)
    j_me = (cx + side) % 2 + 2 * ((cy + side) % 2) + 4 * ((cz + side) % 2)

    def turn(t):
        return ((cx + t) % 4) // 2 + 2 * (((cy + t) % 4) // 2)

    other = 1 - side

    def in_copy(i):
        src, dst = ((hid_h, hid), (again_h, again), (fgain_h, fgain), (freq_h, freq))[i]
        return pltpu.make_async_copy(src, dst, i_sem.at[i])

    def kv_copy(i, c):
        col = pl.multiple_of(i * 1024 + side * 512, 128)
        rows = pl.ds(c * KVC, KVC)
        return pltpu.make_async_copy(wkv.at[0, rows, pl.ds(col, 512)], wkv_b.at[i, rows], kv_sem.at[i, c])

    def q_copy(h):
        col = pl.multiple_of(side * DH + h * 384, 128)
        return pltpu.make_async_copy(wq.at[0, :, pl.ds(col, 384)], wq_b.at[h], w_sem.at[h])

    def c_copy(i, h):
        src, dst = (kc, kc_b) if i == 0 else (vc, vc_b)
        return pltpu.make_async_copy(src.at[0, :, side * KVH + h], dst.at[h], c_sem.at[i, h])

    def head_copies(h):
        q_copy(h).start()
        c_copy(0, h).start()
        c_copy(1, h).start()

    def o_copy(n):
        row = pl.multiple_of(side * DH, 128)
        return pltpu.make_async_copy(wo.at[0, pl.ds(row, DH), pl.ds(pl.multiple_of(n * 512, 128), 512)], wo_b.at[n], wo_sem.at[n])

    def f_copy(i):
        row = pl.multiple_of(side * DH, 128)
        src = wg if i == 0 else wu
        return pltpu.make_async_copy(src.at[0, pl.ds(row, DH), :], wgu_b.at[:, pl.ds(i * FFC, FFC)], f_sem.at[i])

    wd_own = pltpu.make_async_copy(wd.at[0, :, pl.ds(pl.multiple_of(j_me * NC, 128), NC)], wd_b.at[j_me], wd_sem)

    for i in range(4):
        in_copy(i).start()
    for c in range(D // KVC):
        kv_copy(0, c).start()
    for c in range(D // KVC):
        kv_copy(1, c).start()

    barrier = pltpu.get_barrier_semaphore()

    def pair(c):
        return (c + 1 + 2 * ((c + side) % 2)) % 4

    def block_peer(k):
        px = pair(cx) if k % 2 else cx
        py = pair(cy) if (k // 2) % 2 else cy
        pz = pair(cz) if k // 4 else cz
        return flat(px, py, pz), (px + side) % 2 + 2 * ((py + side) % 2) + 4 * ((pz + side) % 2)

    def greet(d, t):
        pl.semaphore_signal(barrier, inc=1, device_id=(0, d, t), device_id_type=MESH)

    with jax.named_scope("greet"):
        greet(dev, other)
        greet(block_peer(GRP - 1)[0], side)
        for i in range(1, 64):
            ix, iy, iz = coords(i)
            if not (ix and iy and iz):
                greet(flat((cx + ix) % 4, (cy + iy) % 4, (cz + iz) % 4), side)
    greeted = 38

    with jax.named_scope("inwait"):
        for i in range(4):
            in_copy(i).wait()

    with jax.named_scope("tables"):
        rowb = lax.broadcasted_iota(jnp.int32, (8, 128), 0)
        lv = jnp.zeros((8, 128), jnp.int32)
        for b in range(8):
            lv = jnp.where(rowb == b, lens[b], lv)
        angle = lv.astype(F32) * freq[...]
        lane = lax.broadcasted_iota(jnp.int32, (8, 128), 1)
        sin = jnp.sin(angle)
        tab[0] = jnp.cos(angle)
        tab[1] = jnp.where(lane < 64, -sin, sin)
        lens_v[...] = jnp.concatenate([lv, lv, lv], axis=0)

    def rotary(v):
        return v * tab[0] + pltpu.roll(v, 64, axis=1) * tab[1]

    with jax.named_scope("norm"):
        xf = hid[...].astype(F32)
        inv = lax.rsqrt(jnp.mean(xf * xf, axis=-1, keepdims=True) + EPS)
        a_b[...] = (xf * inv * again[...]).astype(BF16)

    for i in range(2):
        with jax.named_scope("kvwait"):
            for c in range(D // KVC):
                kv_copy(i, c).wait()
        head_copies(2 * i)
        head_copies(2 * i + 1)
        with jax.named_scope("kvdot"):
            kv = jnp.dot(a_b[...], wkv_b[i], preferred_element_type=F32)
            for h in range(KVH):
                v = kv[:, h * HEAD:(h + 1) * HEAD]
                if i == 0:
                    v = rotary(v)
                kv_b[i, h] = v.astype(BF16).astype(F32)

    rowm = lax.broadcasted_iota(jnp.int32, (24, SEQ), 0) % 8
    rowv = lax.broadcasted_iota(jnp.int32, (24, HEAD), 0) % 8
    pos = lax.broadcasted_iota(jnp.int32, (24, SEQ), 1)
    scale = HEAD ** -0.5

    def attend(h, c):
        with jax.named_scope("qwait"):
            q_copy(h).wait()

        @pl.when(h < 3)
        def _():
            o_copy(2 * h).start()
            o_copy(2 * h + 1).start()

        with jax.named_scope("qdot"):
            q = jnp.dot(a_b[...], wq_b[h], preferred_element_type=F32)
            qf = jnp.concatenate([rotary(q[:, g * HEAD:(g + 1) * HEAD]) for g in range(GROUP)], axis=0)
            qb = qf.astype(BF16)
        k_new = kv_b[0, h]
        v_new = kv_b[1, h]
        k3 = jnp.concatenate([k_new, k_new, k_new], axis=0)
        v3 = jnp.concatenate([v_new, v_new, v_new], axis=0)
        self_score = jnp.sum(qb.astype(F32) * k3, axis=-1, keepdims=True) * scale
        with jax.named_scope("cwait"):
            c_copy(0, h).wait()
            c_copy(1, h).wait()
        with jax.named_scope("mix"):
            s = jnp.zeros((24, SEQ), F32)
            for b in range(8):
                sb = lax.dot_general(qb, kc_b[h, b], (((1,), (1,)), ((), ())), preferred_element_type=F32)
                s = jnp.where(rowm == b, sb, s)
            limit = lens_v[...]
            limit = jnp.concatenate([limit, limit], axis=1)
            s = jnp.where(pos < limit, s * scale, -1e30)
            top = jnp.maximum(jnp.max(s, axis=-1, keepdims=True), self_score)
            e = jnp.exp(s - top)
            es = jnp.exp(self_score - top)
            total = jnp.sum(e, axis=-1, keepdims=True) + es
            eb = e.astype(BF16)
            m = jnp.zeros((24, HEAD), F32)
            for b in range(8):
                mb = jnp.dot(eb, vc_b[h, b], preferred_element_type=F32)
                m = jnp.where(rowv == b, mb, m)
            m = m + es.astype(BF16).astype(F32) * v3
            o = m / total
            for g in range(GROUP):
                o_b[h, :, g * HEAD:(g + 1) * HEAD] = o[g * 8:(g + 1) * 8].astype(BF16)
        return c

    lax.fori_loop(0, 2, attend, 0)
    with jax.named_scope("barrier"):
        pl.semaphore_wait(barrier, greeted)

    def wd_copy(k):
        peer, j = block_peer(k)
        return pltpu.make_async_remote_copy(
            src_ref=wd.at[0, :, pl.ds(pl.multiple_of(j * NC, 128), NC)], dst_ref=wd_b.at[j_me],
            send_sem=wds_sem.at[k], recv_sem=wdr_sem.at[k], device_id=(0, peer, side), device_id_type=MESH)

    with jax.named_scope("wdsend"):
        for k in range(1, GRP):
            wd_copy(k).start()

    lax.fori_loop(2, KVH, attend, 0)

    f_copy(0).start()
    f_copy(1).start()
    wd_own.start()

    def p_copy(n):
        return pltpu.make_async_remote_copy(
            src_ref=p_own.at[n], dst_ref=p_oth.at[n], send_sem=ps_sem.at[n], recv_sem=pr_sem.at[n],
            device_id=(0, dev, other), device_id_type=MESH)

    o_all = jnp.concatenate([o_b[h] for h in range(KVH)], axis=1)

    def project(n, c):
        o_copy(n).wait()
        p_own[n] = jnp.dot(o_all, wo_b[n], preferred_element_type=F32)
        p_copy(n).start()
        return c

    with jax.named_scope("project"):
        lax.fori_loop(0, 6, project, 0)

    with jax.named_scope("x1"):
        ssq = jnp.zeros((8, 1), F32)
        for n in range(6):
            p_copy(n).wait_recv()
            v = hid[:, n * 512:(n + 1) * 512].astype(F32) + (p_own[n] + p_oth[n])
            v = v.astype(BF16).astype(F32)
            x1f[n] = v
            ssq = ssq + jnp.sum(v * v, axis=-1, keepdims=True)
        inv1 = lax.rsqrt(ssq / D + EPS)

        at = []
        for q in range(3):
            ring, plane = ring_slot(q, dev)
            row, col = plane // 4, plane % 4
            at.append((ring, row, col))
            v = x1f[side * 3 + q] * inv1 * fgain[side * 3 + q]
            hbuf[q, ring, row, col] = v.astype(BF16)

    with jax.named_scope("ag1send"):
        for i in ORDER:
            for j in ORDER:
                if i or j:
                    for q in range(3):
                        ring, row, col = at[q]
                        to = ((row + i) % 4) * 4 + (col + j) % 4
                        pltpu.make_async_remote_copy(
                            src_ref=hbuf.at[q, ring, row, col], dst_ref=hbuf.at[q, ring, row, col],
                            send_sem=a1s.at[q], recv_sem=a1r.at[q, (4 - i) % 4],
                            device_id=(0, chip_at(q, ring, to), side), device_id_type=MESH).start()

    def a2_copy(q, g, step, src, sem):
        ring, row, col = at[q]
        part = hbuf.at[q, src, (row + ORDER[g]) % 4]
        return pltpu.make_async_remote_copy(
            src_ref=part, dst_ref=part, send_sem=a2s.at[q], recv_sem=sem,
            device_id=(0, chip_at(q, (ring + step) % 4, row * 4 + col), side), device_id_type=MESH)

    def own_row(g):
        for q in range(3):
            n = 3 if g == 0 else 4
            some = hbuf.at[q, 0, 0, pl.ds(0, n)]
            pltpu.make_async_copy(some, some, a1r.at[q, ORDER[g]]).wait()
            ring = at[q][0]
            a2_copy(q, g, 1, ring, a2r.at[q, 0, g]).start()
            a2_copy(q, g, 3, ring, a2r.at[q, 1, g]).start()

    def recv_row(q, sem):
        some = hbuf.at[q, 0, 0]
        pltpu.make_async_copy(some, some, sem).wait()

    def pass_row(g):
        for q in range(3):
            ring = at[q][0]
            if g in (0, 3):
                recv_row(q, a2r.at[q, 0, g])
                a2_copy(q, g, 1, (ring + 3) % 4, a2f.at[q, g]).start()
            else:
                recv_row(q, a2r.at[q, 1, g])
                a2_copy(q, g, 3, (ring + 1) % 4, a2f.at[q, g]).start()

    for step, g in ((own_row, 0), (own_row, 1), (own_row, 2), (own_row, 3), (pass_row, 0), (pass_row, 1), (pass_row, 2), (pass_row, 3)):
        with jax.named_scope(f"{step.__name__}{g}"):
            step(g)
    with jax.named_scope("ag2wait"):
        for g in range(4):
            for q in range(3):
                recv_row(q, a2r.at[q, 1 if g in (0, 3) else 0, g])
        for g in range(4):
            for q in range(3):
                recv_row(q, a2f.at[q, g])

    f_copy(0).wait()
    f_copy(1).wait()

    def arrange(half, r):
        first = half * 32 + ((r + turn(half)) % CHUNKS) * (32 // CHUNKS)
        for i in range(16 // CHUNKS):
            slots = [[ring_slot(q, first + 2 * i + t) for t in range(2)] for q in range(3)]
            for q in range(3):
                vs = [hbuf[q, ring, plane // 4, plane % 4].astype(F32) for ring, plane in slots[q]]
                h2[r % 2, i * 16:(i + 1) * 16, q * PART:(q + 1) * PART] = jnp.concatenate(vs, axis=0).astype(BF16)
        return h2[r % 2]

    def g_copy(r):
        return pltpu.make_async_remote_copy(
            src_ref=gu_o.at[r], dst_ref=gu_r.at[r], send_sem=gs_sem.at[r], recv_sem=gr_sem.at[r],
            device_id=(0, dev, other), device_id_type=MESH)

    def u_copy(k, r):
        peer, _ = block_peer(k)
        return pltpu.make_async_remote_copy(
            src_ref=ubuf.at[j_me, r], dst_ref=ubuf.at[j_me, r], send_sem=us_sem.at[k, r], recv_sem=ur_sem.at[k, r],
            device_id=(0, peer, side), device_id_type=MESH)

    for r in range(CHUNKS + 1):
        if r < CHUNKS:
            with jax.named_scope("gateup"):
                gu_o[r] = jnp.dot(arrange(other, r), wgu_b[...], preferred_element_type=F32)
                g_copy(r).start()
                gu_m[r] = jnp.dot(arrange(side, r), wgu_b[...], preferred_element_type=F32)
        if r >= 1:
            with jax.named_scope("uact"):
                g_copy(r - 1).wait_recv()
                both = gu_m[r - 1] + gu_r[r - 1]
                gate = both[:, :FFC]
                up = both[:, FFC:]
                ubuf[j_me, r - 1] = (gate * jax.nn.sigmoid(gate) * up).astype(BF16)
                for k in range(1, GRP):
                    u_copy(k, r - 1).start()

    wd_own.wait()
    with jax.named_scope("wdwait"):
        for k in range(1, GRP):
            wd_copy(k).wait_recv()

    here = side == dev // 32
    per = 64 // CHUNKS

    def finish(r, c):
        with jax.named_scope("uwait"):
            for k in range(1, GRP):
                u_copy(k, r).wait_recv()
        with jax.named_scope("down"):
            u_all = jnp.concatenate([ubuf[j, r] for j in range(GRP)], axis=1)
            y = jnp.dot(u_all, wd_b[...].reshape(GRP * FFC, NC), preferred_element_type=F32)
            base = ((r + turn(side)) % CHUNKS) * per
            for i in range(per // 2):
                ysend[base + 2 * i] = y[i * 8:i * 8 + 4]
                ysend[base + 2 * i + 1] = y[i * 8 + 4:i * 8 + 8]

        def give(i, c):
            k = base + (i + me) % per
            d = side * 32 + k // 2
            t = k % 2

            @pl.when(jnp.logical_or(d != dev, t != side))
            def _():
                pltpu.make_async_remote_copy(
                    src_ref=ysend.at[k], dst_ref=yrecv.at[dev], send_sem=ys_sem, recv_sem=yr_sem,
                    device_id=(0, d, t), device_id_type=MESH).start()
            return c

        with jax.named_scope("give"):
            lax.fori_loop(0, per, give, 0, unroll=True)
        return c

    lax.fori_loop(0, CHUNKS, finish, 0)

    @pl.when(here)
    def _():
        yrecv[dev] = ysend[(dev % 32) * 2 + side]

    def wait_blocks(ref, sem):
        @pl.when(here)
        def _():
            pltpu.make_async_copy(ref.at[pl.ds(0, 63)], ref.at[pl.ds(0, 63)], sem).wait()

        @pl.when(jnp.logical_not(here))
        def _():
            pltpu.make_async_copy(ref, ref, sem).wait()

    with jax.named_scope("yrwait"):
        wait_blocks(yrecv, yr_sem)
    with jax.named_scope("final"):
        x1 = jnp.concatenate([x1f[n] for n in range(6)], axis=1)
        x1 = jnp.where(side == 0, x1[0:4], x1[4:8])
        sums = []
        for j in range(GRP):
            acc = None
            for c in range(N_DEV):
                x, y, z = coords(c)
                if (x % 2) + 2 * (y % 2) + 4 * (z % 2) == j:
                    acc = yrecv[c] if acc is None else acc + yrecv[c]
            sums.append(acc)
        for j in range(GRP):
            y = jnp.where(dev // 32 == 0, sums[j], sums[GRP - 1 - j])
            out[:, j * NC:(j + 1) * NC] = (x1[:, j * NC:(j + 1) * NC] + y.astype(BF16).astype(F32)).astype(BF16)

    with jax.named_scope("drain"):
        for k in range(1, GRP):
            wd_copy(k).wait_send()
            for r in range(CHUNKS):
                u_copy(k, r).wait_send()
        for n in range(6):
            p_copy(n).wait_send()
        for q in range(3):
            some = wkv_b.at[0, pl.ds(0, 15 * 8)]
            pltpu.make_async_copy(some, some, a1s.at[q]).wait()
            most = hbuf.at[q, pl.ds(0, 3)]
            pltpu.make_async_copy(most, most, a2s.at[q]).wait()
        for r in range(CHUNKS):
            g_copy(r).wait_send()
        wait_blocks(ysend, ys_sem)


def solution(mesh):
    batch_axes = ('inst', 'dev')
    in_specs = (
        P(batch_axes, None),
        P(batch_axes),
        P(None, batch_axes, None, None, None),
        P(None, batch_axes, None, None, None),
        P(), P(), P(), P(), P(),
        P(None, None, 'dev'),
        P(None, None, 'dev'),
        P(None, 'dev', None),
    )
    out_specs = P(('inst', 'dev', 'side'), None)
    half = HEAD // 2
    freqs = (ROPE_BASE ** (-np.arange(half, dtype=np.float64) / half)).astype(np.float32)
    freqs = np.concatenate([freqs, freqs])[None]

    def device_fn(hidden, cache_len, k_cache, v_cache, w_q, w_kv, w_o, attn_gain, ffn_gain, w_gate, w_up, w_down):
        vmem = pl.BlockSpec(memory_space=pltpu.VMEM)
        hbm = pl.BlockSpec(memory_space=pl.ANY)
        dma = pltpu.SemaphoreType.DMA
        return pl.pallas_call(
            body,
            out_shape=jax.ShapeDtypeStruct((4, D), BF16),
            in_specs=[pl.BlockSpec(memory_space=pltpu.SMEM)] + [hbm] * 12,
            out_specs=vmem,
            scratch_shapes=[
                pltpu.VMEM((8, D), BF16),
                pltpu.VMEM((1, D), F32),
                pltpu.VMEM((6, 1, 512), F32),
                pltpu.VMEM((1, HEAD), F32),
                pltpu.VMEM((KVH, D, 384), BF16),
                pltpu.VMEM((2, D, 512), BF16),
                pltpu.VMEM((6, DH, 512), BF16),
                pltpu.VMEM((KVH, 8, SEQ, HEAD), BF16),
                pltpu.VMEM((KVH, 8, SEQ, HEAD), BF16),
                pltpu.VMEM((DH, 2 * FFC), BF16),
                pltpu.VMEM((GRP, FFC, NC), BF16),
                pltpu.VMEM((8, D), BF16),
                pltpu.VMEM((2, KVH, 8, HEAD), F32),
                pltpu.VMEM((KVH, 8, 384), BF16),
                pltpu.VMEM((6, 8, 512), F32),
                pltpu.VMEM((6, 8, 512), F32),
                pltpu.VMEM((6, 8, 512), F32),
                pltpu.VMEM((3, 4, 4, 4, 8, PART), BF16),
                pltpu.VMEM((2, CH, DH), BF16),
                pltpu.VMEM((CHUNKS, CH, 2 * FFC), F32),
                pltpu.VMEM((CHUNKS, CH, 2 * FFC), F32),
                pltpu.VMEM((CHUNKS, CH, 2 * FFC), F32),
                pltpu.VMEM((GRP, CHUNKS, CH, FFC), BF16),
                pltpu.VMEM((64, 4, NC), F32),
                pltpu.VMEM((64, 4, NC), F32),
                pltpu.VMEM((2, 8, 128), F32),
                pltpu.VMEM((24, 128), jnp.int32),
                dma((4,)), dma((KVH,)), dma((2, D // KVC)), dma((2, KVH)), dma((6,)), dma((2,)), dma, dma((GRP,)), dma((GRP,)),
                dma((6,)), dma((6,)), dma((3,)), dma((3, 4)), dma((3,)), dma((3, 2, 4)), dma((3, 4)), dma((CHUNKS,)), dma((CHUNKS,)),
                dma((GRP, CHUNKS)), dma((GRP, CHUNKS)), dma, dma,
            ],
            compiler_params=pltpu.CompilerParams(
                collective_id=0, has_side_effects=True, vmem_limit_bytes=60 * 1024 * 1024),
            name="decode_layer",
        )(cache_len, hidden, attn_gain, ffn_gain.reshape(6, 1, 512), jnp.asarray(freqs),
          k_cache, v_cache, w_q, w_kv, w_o, w_gate, w_up, w_down)

    return jax.shard_map(device_fn, mesh=mesh, in_specs=in_specs, out_specs=out_specs, check_vma=False)
```

time: 396 us -> 51 us (0.13)
  waiting for transfers between devices: 362 us -> 0 us
  Pallas kernels: 0 us -> 49.5 us
  between operations: 13.4 us -> 0.01 us
  matrix products: 10.6 us -> 0 us
  starting transfers between devices: 6.02 us -> 0 us
    reduce_scatter x1 -> x0, waiting for transfers between devices: 222 us -> none  [device_fn(): summed = lax.psum_scatter(part_sum, 'dev', scatter_dimension=0, tiled=True)]
    ppermute x2 -> x0, waiting for transfers between devices: 72 us -> none  [the longest x1 71.2 us: device_fn(): sent = lax.ppermute(x_pair, 'side', to_ffn)]
    all_gather x1 -> x0, waiting for transfers between devices: 67.4 us -> none  [device_fn(): h_all = lax.all_gather(h_rows, 'dev', axis=0, tiled=True)]
    pallas_call x0 -> x1, Pallas kernels: none -> 49.5 us  [device_fn(): pl.pallas_call(body, out_shape=jax.ShapeDtypeStruct((4, D), BF16), in_spe...]
    dot_general x2 -> x0, matrix products: 10.6 us -> none  [the longest x1 7.43 us: ffn_partial(): return jnp.dot(act_rows, down_weight, preferred_element_type=jnp.float32)]
    ppermute x2 -> x0, starting transfers between devices: 5.97 us -> none  [the longest x1 4.56 us: device_fn(): back = lax.ppermute(x_ffn[:rows], 'side', to_attn)]
  transfers between devices with their start and end apart: 4 -> 0, of which waited for: 4 -> 0; matrix products, arithmetic and copies ran while one was open for 0% -> 0% of each run, Pallas kernels for 0% -> 0%
where the time goes in v2:
time: 51 us; the launch traced here: 50.9 us
  Pallas kernels  49.5 us (97%)
  local copies, waits for them, and re-layouts  1.36 us (3%)
    pallas_call x1, Pallas kernels, device_fn(): pl.pallas_call(body, out_shape=jax.ShapeDtypeStruct((4, D), BF16), in_spe...  49.5 us
    unnamed x1, local copies, waits for them, and re-layouts  1.36 us

profile of v2, /device:TPU:1, one launch (start us, length us, event | category | flops | bytes accessed | tf_op | source)
XLA Modules:
  0.0 50.9 jit_solution(16561716253050200065)
XLA Ops:
  0.0 49.5 %decode_layer.1 = bf16[4,3072]{1,0:T(4,128)(2,1)} custom-call(s32[8]{0:T(128)} %lens.1, bf16[8,3072]{1,0:T(8,128)(2,1)} %hid_h.1, f32[1,3072]{1,0:T(1,128)} %again_h.1, f32[6,1,512]{2,1,0:T(1,128)} %bitcast.1, f32[1,128]{1,0:T(1,128)} %constant.2.clone.freq_h, bf16[1,8,8,256,128]{4,3,2,1,0:T(8,128)(2,1)} %kc.1, bf16[1,8,8,256,128]{4,3,2,1,0:T(8,128)(2,1)} %vc.1, ...), custom_call_target="tpu_custom_call" | custom-call | tf_op jit(solution)/shard_map/decode_layer/pallas_call | solution.py:477
  49.5 1.4 %copy.15 = bf16[4,3072]{1,0:T(4,128)(2,1)} copy(bf16[4,3072]{1,0:T(4,128)(2,1)} %decode_layer.1) | data formatting | bytes 49152

commit v3 on v2

--- a/solution.py
+++ b/solution.py
@@ -15,7 +15,7 @@
 N_DEV = 64
 D = 3072
 DH = D // 2
-PART = 512
+PART = D // 3
 FFC = 128
 SEQ = 256
 HEAD = 128
@@ -38,37 +38,35 @@
     return z * 16 + y * 4 + x
 
 
-def ring_slot(part, dev):
-    x, y, z = coords(dev)
-    if part == 0:
-        return x, z * 4 + y
-    if part == 1:
-        return y, z * 4 + x
-    return z, y * 4 + x
-
-
-def chip_at(part, ring, plane):
-    if part == 0:
-        return flat(ring, plane % 4, plane // 4)
-    if part == 1:
-        return flat(plane % 4, ring, plane // 4)
-    return flat(plane % 4, plane // 4, ring)
+def ring_slot(part, x, y, z):
+    return ((x, z, y), (y, z, x), (z, y, x))[part]
+
+
+def chip_at(part, ring, row, col):
+    return (flat(ring, col, row), flat(col, ring, row), flat(col, row, ring))[part]
 
 
 def body(lens, hid_h, again_h, fgain_h, freq_h, kc, vc, wq, wkv, wo, wg, wu, wd, out,
          hid, again, fgain, freq,
          wq_b, wkv_b, wo_b, kc_b, vc_b, wgu_b, wd_b, a_b, kv_b, o_b, p_own, p_oth, x1f,
-         hbuf, h2, gu_o, gu_m, gu_r, ubuf, ysend, yrecv, tab, lens_v,
+         hbuf, h2, ubuf, ysend, yrecv, tab, lens_v,
          i_sem, w_sem, kv_sem, c_sem, wo_sem, f_sem, wd_sem, wds_sem, wdr_sem,
-         ps_sem, pr_sem, a1s, a1r, a2s, a2r, a2f, gs_sem, gr_sem, us_sem, ur_sem, ys_sem, yr_sem):
+         ps_sem, pr_sem, a1s, a1r, a2s, a2r, a2f, us_sem, ur_sem, ys_sem, yr_sem):
     dev = lax.axis_index("dev")
     side = lax.axis_index("side")
-    me = dev * 2 + side
     cx, cy, cz = coords(dev)
     j_me = (cx + side) % 2 + 2 * ((cy + side) % 2) + 4 * ((cz + side) % 2)
 
-    def turn(t):
-        return ((cx + t) % 4) // 2 + 2 * (((cy + t) % 4) // 2)
+    source = (cx + cy + cz) % 2 == side
+
+    def quadrant(r):
+        dx, dy = ((1, 1), (1, 0), (0, 1), (0, 0))[r]
+        qx = (((cx + side) % 4) // 2 + dx) % 2
+        qy = (((cy + side) % 4) // 2 + dy) % 2
+        return [(2 * qx + i + 4 - side) % 4 for i in range(2)], [(2 * qy + i + 4 - side) % 4 for i in range(2)]
+
+    def height(x, y, i):
+        return 2 * i + (side + x + y) % 2
 
     other = 1 - side
 
@@ -99,9 +97,8 @@
         return pltpu.make_async_copy(wo.at[0, pl.ds(row, DH), pl.ds(pl.multiple_of(n * 512, 128), 512)], wo_b.at[n], wo_sem.at[n])
 
     def f_copy(i):
-        row = pl.multiple_of(side * DH, 128)
         src = wg if i == 0 else wu
-        return pltpu.make_async_copy(src.at[0, pl.ds(row, DH), :], wgu_b.at[:, pl.ds(i * FFC, FFC)], f_sem.at[i])
+        return pltpu.make_async_copy(src.at[0], wgu_b.at[:, pl.ds(i * FFC, FFC)], f_sem.at[i])
 
     wd_own = pltpu.make_async_copy(wd.at[0, :, pl.ds(pl.multiple_of(j_me * NC, 128), NC)], wd_b.at[j_me], wd_sem)
 
@@ -109,8 +106,6 @@
         in_copy(i).start()
     for c in range(D // KVC):
         kv_copy(0, c).start()
-    for c in range(D // KVC):
-        kv_copy(1, c).start()
 
     barrier = pltpu.get_barrier_semaphore()
 
@@ -138,6 +133,8 @@
     with jax.named_scope("inwait"):
         for i in range(4):
             in_copy(i).wait()
+    for c in range(D // KVC):
+        kv_copy(1, c).start()
 
     with jax.named_scope("tables"):
         rowb = lax.broadcasted_iota(jnp.int32, (8, 128), 0)
@@ -163,8 +160,7 @@
         with jax.named_scope("kvwait"):
             for c in range(D // KVC):
                 kv_copy(i, c).wait()
-        head_copies(2 * i)
-        head_copies(2 * i + 1)
+        head_copies(i)
         with jax.named_scope("kvdot"):
             kv = jnp.dot(a_b[...], wkv_b[i], preferred_element_type=F32)
             for h in range(KVH):
@@ -182,10 +178,14 @@
         with jax.named_scope("qwait"):
             q_copy(h).wait()
 
-        @pl.when(h < 3)
+        @pl.when(h < 2)
         def _():
-            o_copy(2 * h).start()
-            o_copy(2 * h + 1).start()
+            head_copies(h + 2)
+
+        @pl.when(h >= 2)
+        def _():
+            for i in range(3):
+                o_copy(3 * (h - 2) + i).start()
 
         with jax.named_scope("qdot"):
             q = jnp.dot(a_b[...], wq_b[h], preferred_element_type=F32)
@@ -268,38 +268,49 @@
             ssq = ssq + jnp.sum(v * v, axis=-1, keepdims=True)
         inv1 = lax.rsqrt(ssq / D + EPS)
 
-        at = []
-        for q in range(3):
-            ring, plane = ring_slot(q, dev)
-            row, col = plane // 4, plane % 4
-            at.append((ring, row, col))
-            v = x1f[side * 3 + q] * inv1 * fgain[side * 3 + q]
-            hbuf[q, ring, row, col] = v.astype(BF16)
+        at = [ring_slot(q, cx, cy, cz) for q in range(3)]
+
+        @pl.when(source)
+        def _():
+            for n in range(6):
+                ring, row, col = at[n // 2]
+                v = x1f[n] * inv1 * fgain[n]
+                hbuf[n // 2, ring, row, col // 2, :, (n % 2) * 512:(n % 2 + 1) * 512] = v.astype(BF16)
 
     with jax.named_scope("ag1send"):
-        for i in ORDER:
-            for j in ORDER:
-                if i or j:
-                    for q in range(3):
-                        ring, row, col = at[q]
-                        to = ((row + i) % 4) * 4 + (col + j) % 4
-                        pltpu.make_async_remote_copy(
-                            src_ref=hbuf.at[q, ring, row, col], dst_ref=hbuf.at[q, ring, row, col],
-                            send_sem=a1s.at[q], recv_sem=a1r.at[q, (4 - i) % 4],
-                            device_id=(0, chip_at(q, ring, to), side), device_id_type=MESH).start()
+        @pl.when(source)
+        def _():
+            for i in ORDER:
+                for j in ORDER:
+                    if i or j:
+                        for q in range(3):
+                            ring, row, col = at[q]
+                            block = hbuf.at[q, ring, row, col // 2]
+                            pltpu.make_async_remote_copy(
+                                src_ref=block, dst_ref=block, send_sem=a1s.at[q], recv_sem=a1r.at[q, (4 - i) % 4],
+                                device_id=(0, chip_at(q, ring, (row + i) % 4, (col + j) % 4), side),
+                                device_id_type=MESH).start()
 
     def a2_copy(q, g, step, src, sem):
         ring, row, col = at[q]
         part = hbuf.at[q, src, (row + ORDER[g]) % 4]
         return pltpu.make_async_remote_copy(
             src_ref=part, dst_ref=part, send_sem=a2s.at[q], recv_sem=sem,
-            device_id=(0, chip_at(q, (ring + step) % 4, row * 4 + col), side), device_id_type=MESH)
+            device_id=(0, chip_at(q, (ring + step) % 4, row, col), side), device_id_type=MESH)
 
     def own_row(g):
         for q in range(3):
-            n = 3 if g == 0 else 4
-            some = hbuf.at[q, 0, 0, pl.ds(0, n)]
-            pltpu.make_async_copy(some, some, a1r.at[q, ORDER[g]]).wait()
+            if g == 0:
+                @pl.when(source)
+                def _(q=q):
+                    some = hbuf.at[q, 0, 0, 0]
+                    pltpu.make_async_copy(some, some, a1r.at[q, 0]).wait()
+
+                @pl.when(jnp.logical_not(source))
+                def _(q=q):
+                    recv_row(q, a1r.at[q, 0])
+            else:
+                recv_row(q, a1r.at[q, ORDER[g]])
             ring = at[q][0]
             a2_copy(q, g, 1, ring, a2r.at[q, 0, g]).start()
             a2_copy(q, g, 3, ring, a2r.at[q, 1, g]).start()
@@ -332,19 +343,17 @@
     f_copy(0).wait()
     f_copy(1).wait()
 
-    def arrange(half, r):
-        first = half * 32 + ((r + turn(half)) % CHUNKS) * (32 // CHUNKS)
-        for i in range(16 // CHUNKS):
-            slots = [[ring_slot(q, first + 2 * i + t) for t in range(2)] for q in range(3)]
+    def arrange(r):
+        xs, ys = quadrant(r)
+        for i in range(4):
+            y, h = ys[i % 2], i // 2
+            slots = [ring_slot_of(xs[t], y, height(xs[t], y, h)) for t in range(2)]
             for q in range(3):
-                vs = [hbuf[q, ring, plane // 4, plane % 4].astype(F32) for ring, plane in slots[q]]
+                vs = [hbuf[q, ring, row, col // 2].astype(F32) for ring, row, col in (slot[q] for slot in slots)]
                 h2[r % 2, i * 16:(i + 1) * 16, q * PART:(q + 1) * PART] = jnp.concatenate(vs, axis=0).astype(BF16)
-        return h2[r % 2]
-
-    def g_copy(r):
-        return pltpu.make_async_remote_copy(
-            src_ref=gu_o.at[r], dst_ref=gu_r.at[r], send_sem=gs_sem.at[r], recv_sem=gr_sem.at[r],
-            device_id=(0, dev, other), device_id_type=MESH)
+
+    def ring_slot_of(x, y, z):
+        return [ring_slot(q, x, y, z) for q in range(3)]
 
     def u_copy(k, r):
         peer, _ = block_peer(k)
@@ -352,70 +361,68 @@
             src_ref=ubuf.at[j_me, r], dst_ref=ubuf.at[j_me, r], send_sem=us_sem.at[k, r], recv_sem=ur_sem.at[k, r],
             device_id=(0, peer, side), device_id_type=MESH)
 
-    for r in range(CHUNKS + 1):
-        if r < CHUNKS:
-            with jax.named_scope("gateup"):
-                gu_o[r] = jnp.dot(arrange(other, r), wgu_b[...], preferred_element_type=F32)
-                g_copy(r).start()
-                gu_m[r] = jnp.dot(arrange(side, r), wgu_b[...], preferred_element_type=F32)
-        if r >= 1:
-            with jax.named_scope("uact"):
-                g_copy(r - 1).wait_recv()
-                both = gu_m[r - 1] + gu_r[r - 1]
-                gate = both[:, :FFC]
-                up = both[:, FFC:]
-                ubuf[j_me, r - 1] = (gate * jax.nn.sigmoid(gate) * up).astype(BF16)
-                for k in range(1, GRP):
-                    u_copy(k, r - 1).start()
+    for r in range(CHUNKS):
+        with jax.named_scope("gateup"):
+            arrange(r)
+            both = jnp.dot(h2[r % 2], wgu_b[...], preferred_element_type=F32)
+            gate = both[:, :FFC]
+            up = both[:, FFC:]
+            ubuf[j_me, r] = (gate * jax.nn.sigmoid(gate) * up).astype(BF16)
+            for k in range(1, GRP):
+                u_copy(k, r).start()
 
     wd_own.wait()
     with jax.named_scope("wdwait"):
         for k in range(1, GRP):
             wd_copy(k).wait_recv()
 
-    here = side == dev // 32
     per = 64 // CHUNKS
 
-    def finish(r, c):
+    fx, fy, fz = (cx + side) % 2, (cy + side) % 2, cz // 2
+
+    def finish(r):
         with jax.named_scope("uwait"):
             for k in range(1, GRP):
                 u_copy(k, r).wait_recv()
         with jax.named_scope("down"):
             u_all = jnp.concatenate([ubuf[j, r] for j in range(GRP)], axis=1)
             y = jnp.dot(u_all, wd_b[...].reshape(GRP * FFC, NC), preferred_element_type=F32)
-            base = ((r + turn(side)) % CHUNKS) * per
             for i in range(per // 2):
-                ysend[base + 2 * i] = y[i * 8:i * 8 + 4]
-                ysend[base + 2 * i + 1] = y[i * 8 + 4:i * 8 + 8]
-
-        def give(i, c):
-            k = base + (i + me) % per
-            d = side * 32 + k // 2
-            t = k % 2
-
-            @pl.when(jnp.logical_or(d != dev, t != side))
-            def _():
-                pltpu.make_async_remote_copy(
-                    src_ref=ysend.at[k], dst_ref=yrecv.at[dev], send_sem=ys_sem, recv_sem=yr_sem,
-                    device_id=(0, d, t), device_id_type=MESH).start()
-            return c
-
+                ysend[r * per + 2 * i] = y[i * 8:i * 8 + 4]
+                ysend[r * per + 2 * i + 1] = y[i * 8 + 4:i * 8 + 8]
         with jax.named_scope("give"):
-            lax.fori_loop(0, per, give, 0, unroll=True)
-        return c
-
-    lax.fori_loop(0, CHUNKS, finish, 0)
-
-    @pl.when(here)
+            xs, ys = quadrant(r)
+            ax, ay, az = [(a + fx) % 2 for a in range(2)], [(a + fy) % 2 for a in range(2)], [(a + fz) % 2 for a in range(2)]
+            px = [jnp.where(a == 0, xs[0], xs[1]) for a in ax]
+            py = [jnp.where(a == 0, ys[0], ys[1]) for a in ay]
+            for i in range(per):
+                a, b, c, t = i % 2, (i // 2) % 2, 1 - (i // 4) % 2, i // 8
+                k = 2 * (ax[a] + 2 * ay[b] + 4 * az[c]) + t
+                d = flat(px[a], py[b], height(px[a], py[b], az[c]))
+
+                def start(k=k, d=d, t=t):
+                    pltpu.make_async_remote_copy(
+                        src_ref=ysend.at[r * per + k], dst_ref=yrecv.at[dev], send_sem=ys_sem, recv_sem=yr_sem,
+                        device_id=(0, d, t), device_id_type=MESH).start()
+
+                if r == CHUNKS - 1 and not (a or b or c):
+                    pl.when(jnp.logical_not(jnp.logical_and(source, side == t)))(start)
+                else:
+                    start()
+
+    for r in range(CHUNKS):
+        finish(r)
+
+    @pl.when(source)
     def _():
-        yrecv[dev] = ysend[(dev % 32) * 2 + side]
+        yrecv[dev] = ysend[(CHUNKS - 1) * per + 2 * (fx + 2 * fy + 4 * fz) + side]
 
     def wait_blocks(ref, sem):
-        @pl.when(here)
+        @pl.when(source)
         def _():
             pltpu.make_async_copy(ref.at[pl.ds(0, 63)], ref.at[pl.ds(0, 63)], sem).wait()
 
-        @pl.when(jnp.logical_not(here))
+        @pl.when(jnp.logical_not(source))
         def _():
             pltpu.make_async_copy(ref, ref, sem).wait()
 
@@ -433,7 +440,7 @@
                     acc = yrecv[c] if acc is None else acc + yrecv[c]
             sums.append(acc)
         for j in range(GRP):
-            y = jnp.where(dev // 32 == 0, sums[j], sums[GRP - 1 - j])
+            y = jnp.where((cx + cy + cz) % 2 == 0, sums[j], sums[GRP - 1 - j])
             out[:, j * NC:(j + 1) * NC] = (x1[:, j * NC:(j + 1) * NC] + y.astype(BF16).astype(F32)).astype(BF16)
 
     with jax.named_scope("drain"):
@@ -444,12 +451,12 @@
         for n in range(6):
             p_copy(n).wait_send()
         for q in range(3):
-            some = wkv_b.at[0, pl.ds(0, 15 * 8)]
-            pltpu.make_async_copy(some, some, a1s.at[q]).wait()
+            @pl.when(source)
+            def _(q=q):
+                some = wkv_b.at[0, pl.ds(0, 15 * 16)]
+                pltpu.make_async_copy(some, some, a1s.at[q]).wait()
             most = hbuf.at[q, pl.ds(0, 3)]
             pltpu.make_async_copy(most, most, a2s.at[q]).wait()
-        for r in range(CHUNKS):
-            g_copy(r).wait_send()
         wait_blocks(ysend, ys_sem)
 
 
@@ -489,7 +496,7 @@
                 pltpu.VMEM((6, DH, 512), BF16),
                 pltpu.VMEM((KVH, 8, SEQ, HEAD), BF16),
                 pltpu.VMEM((KVH, 8, SEQ, HEAD), BF16),
-                pltpu.VMEM((DH, 2 * FFC), BF16),
+                pltpu.VMEM((D, 2 * FFC), BF16),
                 pltpu.VMEM((GRP, FFC, NC), BF16),
                 pltpu.VMEM((8, D), BF16),
                 pltpu.VMEM((2, KVH, 8, HEAD), F32),
@@ -497,18 +504,15 @@
                 pltpu.VMEM((6, 8, 512), F32),
                 pltpu.VMEM((6, 8, 512), F32),
                 pltpu.VMEM((6, 8, 512), F32),
-                pltpu.VMEM((3, 4, 4, 4, 8, PART), BF16),
-                pltpu.VMEM((2, CH, DH), BF16),
-                pltpu.VMEM((CHUNKS, CH, 2 * FFC), F32),
-                pltpu.VMEM((CHUNKS, CH, 2 * FFC), F32),
-                pltpu.VMEM((CHUNKS, CH, 2 * FFC), F32),
+                pltpu.VMEM((3, 4, 4, 2, 8, PART), BF16),
+                pltpu.VMEM((2, CH, D), BF16),
                 pltpu.VMEM((GRP, CHUNKS, CH, FFC), BF16),
                 pltpu.VMEM((64, 4, NC), F32),
                 pltpu.VMEM((64, 4, NC), F32),
                 pltpu.VMEM((2, 8, 128), F32),
                 pltpu.VMEM((24, 128), jnp.int32),
                 dma((4,)), dma((KVH,)), dma((2, D // KVC)), dma((2, KVH)), dma((6,)), dma((2,)), dma, dma((GRP,)), dma((GRP,)),
-                dma((6,)), dma((6,)), dma((3,)), dma((3, 4)), dma((3,)), dma((3, 2, 4)), dma((3, 4)), dma((CHUNKS,)), dma((CHUNKS,)),
+                dma((6,)), dma((6,)), dma((3,)), dma((3, 4)), dma((3,)), dma((3, 2, 4)), dma((3, 4)),
                 dma((GRP, CHUNKS)), dma((GRP, CHUNKS)), dma, dma,
             ],
             compiler_params=pltpu.CompilerParams(

time: 51 us -> 49.5 us (0.971)
  Pallas kernels: 49.5 us -> 48 us
    pallas_call x1, Pallas kernels: 49.5 us -> 48 us  [device_fn(): pl.pallas_call(body, out_shape=jax.ShapeDtypeStruct((4, D), BF16), in_spe...]
where the time goes in v3:
time: 49.5 us; the launch traced here: 49.4 us
  Pallas kernels  48 us (97%)
  local copies, waits for them, and re-layouts  1.36 us (3%)
    pallas_call x1, Pallas kernels, device_fn(): pl.pallas_call(body, out_shape=jax.ShapeDtypeStruct((4, D), BF16), in_spe...  48 us
    unnamed x1, local copies, waits for them, and re-layouts  1.36 us

profile of v3, /device:TPU:1, one launch (start us, length us, event | category | flops | bytes accessed | tf_op | source)
XLA Modules:
  0.0 49.4 jit_solution(9325039315979444510)
XLA Ops:
  0.0 48.0 %decode_layer.1 = bf16[4,3072]{1,0:T(4,128)(2,1)} custom-call(s32[8]{0:T(128)} %lens.1, bf16[8,3072]{1,0:T(8,128)(2,1)} %hid_h.1, f32[1,3072]{1,0:T(1,128)} %again_h.1, f32[6,1,512]{2,1,0:T(1,128)} %bitcast.1, f32[1,128]{1,0:T(1,128)} %constant.2.clone.freq_h, bf16[1,8,8,256,128]{4,3,2,1,0:T(8,128)(2,1)} %kc.1, bf16[1,8,8,256,128]{4,3,2,1,0:T(8,128)(2,1)} %vc.1, ...), custom_call_target="tpu_custom_call" | custom-call | tf_op jit(solution)/shard_map/decode_layer/pallas_call | solution.py:484
  48.0 1.4 %copy.15 = bf16[4,3072]{1,0:T(4,128)(2,1)} copy(bf16[4,3072]{1,0:T(4,128)(2,1)} %decode_layer.1) | data formatting | bytes 49152

commit v4 on v3

--- a/solution.py
+++ b/solution.py
@@ -24,7 +24,7 @@
 GRP = 8
 NC = D // GRP
 ROWS = 256
-CHUNKS = 4
+CHUNKS = 2
 CH = ROWS // CHUNKS
 KVC = 768
 ORDER = (0, 1, 3, 2)
@@ -51,7 +51,7 @@
          wq_b, wkv_b, wo_b, kc_b, vc_b, wgu_b, wd_b, a_b, kv_b, o_b, p_own, p_oth, x1f,
          hbuf, h2, ubuf, ysend, yrecv, tab, lens_v,
          i_sem, w_sem, kv_sem, c_sem, wo_sem, f_sem, wd_sem, wds_sem, wdr_sem,
-         ps_sem, pr_sem, a1s, a1r, a2s, a2r, a2f, us_sem, ur_sem, ys_sem, yr_sem):
+         ps_sem, pr_sem, a1s, a1r, a2s, a2r, us_sem, ur_sem, ys_sem, yr_sem):
     dev = lax.axis_index("dev")
     side = lax.axis_index("side")
     cx, cy, cz = coords(dev)
@@ -59,11 +59,9 @@
 
     source = (cx + cy + cz) % 2 == side
 
-    def quadrant(r):
-        dx, dy = ((1, 1), (1, 0), (0, 1), (0, 0))[r]
-        qx = (((cx + side) % 4) // 2 + dx) % 2
-        qy = (((cy + side) % 4) // 2 + dy) % 2
-        return [(2 * qx + i + 4 - side) % 4 for i in range(2)], [(2 * qy + i + 4 - side) % 4 for i in range(2)]
+    def half(r):
+        qx = (((cx + side) % 4) // 2 + 1 - r) % 2
+        return [(2 * qx + i + 4 - side) % 4 for i in range(2)]
 
     def height(x, y, i):
         return 2 * i + (side + x + y) % 2
@@ -80,12 +78,12 @@
         return pltpu.make_async_copy(wkv.at[0, rows, pl.ds(col, 512)], wkv_b.at[i, rows], kv_sem.at[i, c])
 
     def q_copy(h):
-        col = pl.multiple_of(side * DH + h * 384, 128)
-        return pltpu.make_async_copy(wq.at[0, :, pl.ds(col, 384)], wq_b.at[h], w_sem.at[h])
+        col = pl.multiple_of(side * DH + h * 768, 128)
+        return pltpu.make_async_copy(wq.at[0, :, pl.ds(col, 768)], wq_b.at[h], w_sem.at[h])
 
     def c_copy(i, h):
         src, dst = (kc, kc_b) if i == 0 else (vc, vc_b)
-        return pltpu.make_async_copy(src.at[0, :, side * KVH + h], dst.at[h], c_sem.at[i, h])
+        return pltpu.make_async_copy(src.at[0, :, pl.ds(side * KVH + 2 * h, 2)], dst.at[h], c_sem.at[i, h])
 
     def head_copies(h):
         q_copy(h).start()
@@ -130,11 +128,12 @@
                 greet(flat((cx + ix) % 4, (cy + iy) % 4, (cz + iz) % 4), side)
     greeted = 38
 
+    for c in range(D // KVC):
+        kv_copy(1, c).start()
+
     with jax.named_scope("inwait"):
         for i in range(4):
             in_copy(i).wait()
-    for c in range(D // KVC):
-        kv_copy(1, c).start()
 
     with jax.named_scope("tables"):
         rowb = lax.broadcasted_iota(jnp.int32, (8, 128), 0)
@@ -174,55 +173,53 @@
     pos = lax.broadcasted_iota(jnp.int32, (24, SEQ), 1)
     scale = HEAD ** -0.5
 
-    def attend(h, c):
+    def attend(p):
         with jax.named_scope("qwait"):
-            q_copy(h).wait()
-
-        @pl.when(h < 2)
-        def _():
-            head_copies(h + 2)
-
-        @pl.when(h >= 2)
-        def _():
-            for i in range(3):
-                o_copy(3 * (h - 2) + i).start()
-
+            q_copy(p).wait()
+        for i in range(3):
+            o_copy(3 * p + i).start()
         with jax.named_scope("qdot"):
-            q = jnp.dot(a_b[...], wq_b[h], preferred_element_type=F32)
-            qf = jnp.concatenate([rotary(q[:, g * HEAD:(g + 1) * HEAD]) for g in range(GROUP)], axis=0)
-            qb = qf.astype(BF16)
-        k_new = kv_b[0, h]
-        v_new = kv_b[1, h]
-        k3 = jnp.concatenate([k_new, k_new, k_new], axis=0)
-        v3 = jnp.concatenate([v_new, v_new, v_new], axis=0)
-        self_score = jnp.sum(qb.astype(F32) * k3, axis=-1, keepdims=True) * scale
+            q = jnp.dot(a_b[...], wq_b[p], preferred_element_type=F32)
+            qbs = [jnp.concatenate([rotary(q[:, (h * GROUP + g) * HEAD:(h * GROUP + g + 1) * HEAD]) for g in range(GROUP)], axis=0).astype(BF16)
+                   for h in range(2)]
         with jax.named_scope("cwait"):
-            c_copy(0, h).wait()
-            c_copy(1, h).wait()
+            c_copy(0, p).wait()
+            c_copy(1, p).wait()
         with jax.named_scope("mix"):
-            s = jnp.zeros((24, SEQ), F32)
-            for b in range(8):
-                sb = lax.dot_general(qb, kc_b[h, b], (((1,), (1,)), ((), ())), preferred_element_type=F32)
-                s = jnp.where(rowm == b, sb, s)
             limit = lens_v[...]
             limit = jnp.concatenate([limit, limit], axis=1)
-            s = jnp.where(pos < limit, s * scale, -1e30)
-            top = jnp.maximum(jnp.max(s, axis=-1, keepdims=True), self_score)
-            e = jnp.exp(s - top)
-            es = jnp.exp(self_score - top)
-            total = jnp.sum(e, axis=-1, keepdims=True) + es
-            eb = e.astype(BF16)
-            m = jnp.zeros((24, HEAD), F32)
-            for b in range(8):
-                mb = jnp.dot(eb, vc_b[h, b], preferred_element_type=F32)
-                m = jnp.where(rowv == b, mb, m)
-            m = m + es.astype(BF16).astype(F32) * v3
-            o = m / total
-            for g in range(GROUP):
-                o_b[h, :, g * HEAD:(g + 1) * HEAD] = o[g * 8:(g + 1) * 8].astype(BF16)
-        return c
-
-    lax.fori_loop(0, 2, attend, 0)
+            scores = []
+            for h in range(2):
+                s = jnp.zeros((24, SEQ), F32)
+                for b in range(8):
+                    sb = lax.dot_general(qbs[h], kc_b[p, b, h], (((1,), (1,)), ((), ())), preferred_element_type=F32)
+                    s = jnp.where(rowm == b, sb, s)
+                scores.append(jnp.where(pos < limit, s * scale, -1e30))
+            mixed = []
+            for h in range(2):
+                s = scores[h]
+                k_new = kv_b[0, 2 * p + h]
+                k3 = jnp.concatenate([k_new, k_new, k_new], axis=0)
+                self_score = jnp.sum(qbs[h].astype(F32) * k3, axis=-1, keepdims=True) * scale
+                top = jnp.maximum(jnp.max(s, axis=-1, keepdims=True), self_score)
+                e = jnp.exp(s - top)
+                es = jnp.exp(self_score - top)
+                total = jnp.sum(e, axis=-1, keepdims=True) + es
+                mixed.append((e.astype(BF16), es, total))
+            for h in range(2):
+                eb, es, total = mixed[h]
+                m = jnp.zeros((24, HEAD), F32)
+                for b in range(8):
+                    mb = jnp.dot(eb, vc_b[p, b, h], preferred_element_type=F32)
+                    m = jnp.where(rowv == b, mb, m)
+                v_new = kv_b[1, 2 * p + h]
+                v3 = jnp.concatenate([v_new, v_new, v_new], axis=0)
+                m = m + es.astype(BF16).astype(F32) * v3
+                o = m / total
+                for g in range(GROUP):
+                    o_b[2 * p + h, :, g * HEAD:(g + 1) * HEAD] = o[g * 8:(g + 1) * 8].astype(BF16)
+
+    attend(0)
     with jax.named_scope("barrier"):
         pl.semaphore_wait(barrier, greeted)
 
@@ -236,7 +233,7 @@
         for k in range(1, GRP):
             wd_copy(k).start()
 
-    lax.fori_loop(2, KVH, attend, 0)
+    attend(1)
 
     f_copy(0).start()
     f_copy(1).start()
@@ -291,69 +288,50 @@
                                 device_id=(0, chip_at(q, ring, (row + i) % 4, (col + j) % 4), side),
                                 device_id_type=MESH).start()
 
-    def a2_copy(q, g, step, src, sem):
-        ring, row, col = at[q]
-        part = hbuf.at[q, src, (row + ORDER[g]) % 4]
-        return pltpu.make_async_remote_copy(
-            src_ref=part, dst_ref=part, send_sem=a2s.at[q], recv_sem=sem,
-            device_id=(0, chip_at(q, (ring + step) % 4, row, col), side), device_id_type=MESH)
-
-    def own_row(g):
-        for q in range(3):
-            if g == 0:
-                @pl.when(source)
-                def _(q=q):
-                    some = hbuf.at[q, 0, 0, 0]
-                    pltpu.make_async_copy(some, some, a1r.at[q, 0]).wait()
-
-                @pl.when(jnp.logical_not(source))
-                def _(q=q):
-                    recv_row(q, a1r.at[q, 0])
-            else:
-                recv_row(q, a1r.at[q, ORDER[g]])
-            ring = at[q][0]
-            a2_copy(q, g, 1, ring, a2r.at[q, 0, g]).start()
-            a2_copy(q, g, 3, ring, a2r.at[q, 1, g]).start()
-
     def recv_row(q, sem):
         some = hbuf.at[q, 0, 0]
         pltpu.make_async_copy(some, some, sem).wait()
 
-    def pass_row(g):
+    def own_row(g, q):
+        if g == 0:
+            @pl.when(source)
+            def _():
+                some = hbuf.at[q, 0, 0, 0]
+                pltpu.make_async_copy(some, some, a1r.at[q, 0]).wait()
+
+            @pl.when(jnp.logical_not(source))
+            def _():
+                recv_row(q, a1r.at[q, 0])
+        else:
+            recv_row(q, a1r.at[q, ORDER[g]])
+        ring, row, col = at[q]
+        part = hbuf.at[q, ring, (row + ORDER[g]) % 4]
+        for step in (2, 1, 3):
+            pltpu.make_async_remote_copy(
+                src_ref=part, dst_ref=part, send_sem=a2s.at[q], recv_sem=a2r.at[q],
+                device_id=(0, chip_at(q, (ring + step) % 4, row, col), side), device_id_type=MESH).start()
+
+    for g in range(4):
+        with jax.named_scope(f"own_row{g}"):
+            for q in range(3):
+                own_row(g, q)
+    with jax.named_scope("ag2wait"):
         for q in range(3):
-            ring = at[q][0]
-            if g in (0, 3):
-                recv_row(q, a2r.at[q, 0, g])
-                a2_copy(q, g, 1, (ring + 3) % 4, a2f.at[q, g]).start()
-            else:
-                recv_row(q, a2r.at[q, 1, g])
-                a2_copy(q, g, 3, (ring + 1) % 4, a2f.at[q, g]).start()
-
-    for step, g in ((own_row, 0), (own_row, 1), (own_row, 2), (own_row, 3), (pass_row, 0), (pass_row, 1), (pass_row, 2), (pass_row, 3)):
-        with jax.named_scope(f"{step.__name__}{g}"):
-            step(g)
-    with jax.named_scope("ag2wait"):
-        for g in range(4):
-            for q in range(3):
-                recv_row(q, a2r.at[q, 1 if g in (0, 3) else 0, g])
-        for g in range(4):
-            for q in range(3):
-                recv_row(q, a2f.at[q, g])
+            most = hbuf.at[q, pl.ds(0, 3)]
+            pltpu.make_async_copy(most, most, a2r.at[q]).wait()
 
     f_copy(0).wait()
     f_copy(1).wait()
 
     def arrange(r):
-        xs, ys = quadrant(r)
-        for i in range(4):
-            y, h = ys[i % 2], i // 2
-            slots = [ring_slot_of(xs[t], y, height(xs[t], y, h)) for t in range(2)]
+        xs = half(r)
+        for i in range(8):
+            y, h = i % 4, i // 4
+            zs = [height(x, y, h) for x in xs]
+            slots = [((xs[t], zs[t], y // 2), (y, zs[t], xs[t] // 2), (zs[t], y, xs[t] // 2)) for t in range(2)]
             for q in range(3):
-                vs = [hbuf[q, ring, row, col // 2].astype(F32) for ring, row, col in (slot[q] for slot in slots)]
+                vs = [hbuf[q, ring, row, col].astype(F32) for ring, row, col in (slot[q] for slot in slots)]
                 h2[r % 2, i * 16:(i + 1) * 16, q * PART:(q + 1) * PART] = jnp.concatenate(vs, axis=0).astype(BF16)
-
-    def ring_slot_of(x, y, z):
-        return [ring_slot(q, x, y, z) for q in range(3)]
 
     def u_copy(k, r):
         peer, _ = block_peer(k)
@@ -378,7 +356,7 @@
 
     per = 64 // CHUNKS
 
-    fx, fy, fz = (cx + side) % 2, (cy + side) % 2, cz // 2
+    fx, fz = (cx + side) % 2, cz // 2
 
     def finish(r):
         with jax.named_scope("uwait"):
@@ -391,14 +369,13 @@
                 ysend[r * per + 2 * i] = y[i * 8:i * 8 + 4]
                 ysend[r * per + 2 * i + 1] = y[i * 8 + 4:i * 8 + 8]
         with jax.named_scope("give"):
-            xs, ys = quadrant(r)
-            ax, ay, az = [(a + fx) % 2 for a in range(2)], [(a + fy) % 2 for a in range(2)], [(a + fz) % 2 for a in range(2)]
+            xs = half(r)
+            ax, ay, az = [(a + fx) % 2 for a in range(2)], [(b + cy) % 4 for b in range(4)], [(c + fz) % 2 for c in range(2)]
             px = [jnp.where(a == 0, xs[0], xs[1]) for a in ax]
-            py = [jnp.where(a == 0, ys[0], ys[1]) for a in ay]
             for i in range(per):
-                a, b, c, t = i % 2, (i // 2) % 2, 1 - (i // 4) % 2, i // 8
-                k = 2 * (ax[a] + 2 * ay[b] + 4 * az[c]) + t
-                d = flat(px[a], py[b], height(px[a], py[b], az[c]))
+                a, b, c, t = i % 2, 3 - (i // 2) % 4, 1 - (i // 8) % 2, i // 16
+                k = 2 * (ax[a] + 2 * ay[b] + 8 * az[c]) + t
+                d = flat(px[a], ay[b], height(px[a], ay[b], az[c]))
 
                 def start(k=k, d=d, t=t):
                     pltpu.make_async_remote_copy(
@@ -415,7 +392,7 @@
 
     @pl.when(source)
     def _():
-        yrecv[dev] = ysend[(CHUNKS - 1) * per + 2 * (fx + 2 * fy + 4 * fz) + side]
+        yrecv[dev] = ysend[(CHUNKS - 1) * per + 2 * (fx + 2 * cy + 8 * fz) + side]
 
     def wait_blocks(ref, sem):
         @pl.when(source)
@@ -491,11 +468,11 @@
                 pltpu.VMEM((1, D), F32),
                 pltpu.VMEM((6, 1, 512), F32),
                 pltpu.VMEM((1, HEAD), F32),
-                pltpu.VMEM((KVH, D, 384), BF16),
+                pltpu.VMEM((2, D, 768), BF16),
                 pltpu.VMEM((2, D, 512), BF16),
                 pltpu.VMEM((6, DH, 512), BF16),
-                pltpu.VMEM((KVH, 8, SEQ, HEAD), BF16),
-                pltpu.VMEM((KVH, 8, SEQ, HEAD), BF16),
+                pltpu.VMEM((2, 8, 2, SEQ, HEAD), BF16),
+                pltpu.VMEM((2, 8, 2, SEQ, HEAD), BF16),
                 pltpu.VMEM((D, 2 * FFC), BF16),
                 pltpu.VMEM((GRP, FFC, NC), BF16),
                 pltpu.VMEM((8, D), BF16),
@@ -511,8 +488,8 @@
                 pltpu.VMEM((64, 4, NC), F32),
                 pltpu.VMEM((2, 8, 128), F32),
                 pltpu.VMEM((24, 128), jnp.int32),
-                dma((4,)), dma((KVH,)), dma((2, D // KVC)), dma((2, KVH)), dma((6,)), dma((2,)), dma, dma((GRP,)), dma((GRP,)),
-                dma((6,)), dma((6,)), dma((3,)), dma((3, 4)), dma((3,)), dma((3, 2, 4)), dma((3, 4)),
+                dma((4,)), dma((2,)), dma((2, D // KVC)), dma((2, 2)), dma((6,)), dma((2,)), dma, dma((GRP,)), dma((GRP,)),
+                dma((6,)), dma((6,)), dma((3,)), dma((3, 4)), dma((3,)), dma((3,)),
                 dma((GRP, CHUNKS)), dma((GRP, CHUNKS)), dma, dma,
             ],
             compiler_params=pltpu.CompilerParams(

time: 49.5 us -> 47.4 us (0.958)
  Pallas kernels: 48 us -> 45.8 us
    pallas_call x1, Pallas kernels: 48 us -> 45.8 us  [device_fn(): pl.pallas_call(body, out_shape=jax.ShapeDtypeStruct((4, D), BF16), in_spe...]
where the time goes in v4:
time: 47.4 us; the launch traced here: 47.2 us
  Pallas kernels  45.8 us (97%)
  local copies, waits for them, and re-layouts  1.36 us (3%)
    pallas_call x1, Pallas kernels, device_fn(): pl.pallas_call(body, out_shape=jax.ShapeDtypeStruct((4, D), BF16), in_spe...  45.8 us
    unnamed x1, local copies, waits for them, and re-layouts  1.36 us

profile of v4, /device:TPU:1, one launch (start us, length us, event | category | flops | bytes accessed | tf_op | source)
XLA Modules:
  0.0 47.2 jit_solution(3734774930517848278)
XLA Ops:
  0.0 45.8 %decode_layer.1 = bf16[4,3072]{1,0:T(4,128)(2,1)} custom-call(s32[8]{0:T(128)} %lens.1, bf16[8,3072]{1,0:T(8,128)(2,1)} %hid_h.1, f32[1,3072]{1,0:T(1,128)} %again_h.1, f32[6,1,512]{2,1,0:T(1,128)} %bitcast.1, f32[1,128]{1,0:T(1,128)} %constant.2.clone.freq_h, bf16[1,8,8,256,128]{4,3,2,1,0:T(8,128)(2,1)} %kc.1, bf16[1,8,8,256,128]{4,3,2,1,0:T(8,128)(2,1)} %vc.1, ...), custom_call_target="tpu_custom_call" | custom-call | tf_op jit(solution)/shard_map/decode_layer/pallas_call | solution.py:461
  45.8 1.4 %copy.15 = bf16[4,3072]{1,0:T(4,128)(2,1)} copy(bf16[4,3072]{1,0:T(4,128)(2,1)} %decode_layer.1) | data formatting | bytes 49152

commit v5 on v4

--- a/solution.py
+++ b/solution.py
@@ -46,8 +46,8 @@
     return (flat(ring, col, row), flat(col, ring, row), flat(col, row, ring))[part]
 
 
-def body(lens, hid_h, again_h, fgain_h, freq_h, kc, vc, wq, wkv, wo, wg, wu, wd, out,
-         hid, again, fgain, freq,
+def body(lens_h, hid_h, again_h, fgain_h, freq_h, kc, vc, wq, wkv, wo, wg, wu, wd, out,
+         lens, hid, again, fgain, freq,
          wq_b, wkv_b, wo_b, kc_b, vc_b, wgu_b, wd_b, a_b, kv_b, o_b, p_own, p_oth, x1f,
          hbuf, h2, ubuf, ysend, yrecv, tab, lens_v,
          i_sem, w_sem, kv_sem, c_sem, wo_sem, f_sem, wd_sem, wds_sem, wdr_sem,
@@ -69,13 +69,13 @@
     other = 1 - side
 
     def in_copy(i):
-        src, dst = ((hid_h, hid), (again_h, again), (fgain_h, fgain), (freq_h, freq))[i]
+        src, dst = ((hid_h, hid), (again_h, again), (fgain_h, fgain), (freq_h, freq), (lens_h, lens))[i]
         return pltpu.make_async_copy(src, dst, i_sem.at[i])
 
     def kv_copy(i, c):
         col = pl.multiple_of(i * 1024 + side * 512, 128)
         rows = pl.ds(c * KVC, KVC)
-        return pltpu.make_async_copy(wkv.at[0, rows, pl.ds(col, 512)], wkv_b.at[i, rows], kv_sem.at[i, c])
+        return pltpu.make_async_copy(wkv.at[0, rows, pl.ds(col, 512)], wkv_b.at[i, rows], kv_sem.at[i])
 
     def q_copy(h):
         col = pl.multiple_of(side * DH + h * 768, 128)
@@ -100,7 +100,7 @@
 
     wd_own = pltpu.make_async_copy(wd.at[0, :, pl.ds(pl.multiple_of(j_me * NC, 128), NC)], wd_b.at[j_me], wd_sem)
 
-    for i in range(4):
+    for i in range(5):
         in_copy(i).start()
     for c in range(D // KVC):
         kv_copy(0, c).start()
@@ -132,7 +132,7 @@
         kv_copy(1, c).start()
 
     with jax.named_scope("inwait"):
-        for i in range(4):
+        for i in range(5):
             in_copy(i).wait()
 
     with jax.named_scope("tables"):
@@ -157,8 +157,7 @@
 
     for i in range(2):
         with jax.named_scope("kvwait"):
-            for c in range(D // KVC):
-                kv_copy(i, c).wait()
+            pltpu.make_async_copy(wkv_b.at[i], wkv_b.at[i], kv_sem.at[i]).wait()
         head_copies(i)
         with jax.named_scope("kvdot"):
             kv = jnp.dot(a_b[...], wkv_b[i], preferred_element_type=F32)
@@ -227,7 +226,7 @@
         peer, j = block_peer(k)
         return pltpu.make_async_remote_copy(
             src_ref=wd.at[0, :, pl.ds(pl.multiple_of(j * NC, 128), NC)], dst_ref=wd_b.at[j_me],
-            send_sem=wds_sem.at[k], recv_sem=wdr_sem.at[k], device_id=(0, peer, side), device_id_type=MESH)
+            send_sem=wds_sem, recv_sem=wdr_sem, device_id=(0, peer, side), device_id_type=MESH)
 
     with jax.named_scope("wdsend"):
         for k in range(1, GRP):
@@ -241,7 +240,7 @@
 
     def p_copy(n):
         return pltpu.make_async_remote_copy(
-            src_ref=p_own.at[n], dst_ref=p_oth.at[n], send_sem=ps_sem.at[n], recv_sem=pr_sem.at[n],
+            src_ref=p_own.at[n], dst_ref=p_oth.at[n], send_sem=ps_sem, recv_sem=pr_sem,
             device_id=(0, dev, other), device_id_type=MESH)
 
     o_all = jnp.concatenate([o_b[h] for h in range(KVH)], axis=1)
@@ -257,8 +256,8 @@
 
     with jax.named_scope("x1"):
         ssq = jnp.zeros((8, 1), F32)
+        pltpu.make_async_copy(p_oth, p_oth, pr_sem).wait()
         for n in range(6):
-            p_copy(n).wait_recv()
             v = hid[:, n * 512:(n + 1) * 512].astype(F32) + (p_own[n] + p_oth[n])
             v = v.astype(BF16).astype(F32)
             x1f[n] = v
@@ -284,7 +283,7 @@
                             ring, row, col = at[q]
                             block = hbuf.at[q, ring, row, col // 2]
                             pltpu.make_async_remote_copy(
-                                src_ref=block, dst_ref=block, send_sem=a1s.at[q], recv_sem=a1r.at[q, (4 - i) % 4],
+                                src_ref=block, dst_ref=block, send_sem=a1s, recv_sem=a1r.at[q, (4 - i) % 4],
                                 device_id=(0, chip_at(q, ring, (row + i) % 4, (col + j) % 4), side),
                                 device_id_type=MESH).start()
 
@@ -308,7 +307,7 @@
         part = hbuf.at[q, ring, (row + ORDER[g]) % 4]
         for step in (2, 1, 3):
             pltpu.make_async_remote_copy(
-                src_ref=part, dst_ref=part, send_sem=a2s.at[q], recv_sem=a2r.at[q],
+                src_ref=part, dst_ref=part, send_sem=a2s, recv_sem=a2r,
                 device_id=(0, chip_at(q, (ring + step) % 4, row, col), side), device_id_type=MESH).start()
 
     for g in range(4):
@@ -316,9 +315,8 @@
             for q in range(3):
                 own_row(g, q)
     with jax.named_scope("ag2wait"):
-        for q in range(3):
-            most = hbuf.at[q, pl.ds(0, 3)]
-            pltpu.make_async_copy(most, most, a2r.at[q]).wait()
+        most = hbuf.at[:, pl.ds(0, 3)]
+        pltpu.make_async_copy(most, most, a2r).wait()
 
     f_copy(0).wait()
     f_copy(1).wait()
@@ -336,7 +334,7 @@
     def u_copy(k, r):
         peer, _ = block_peer(k)
         return pltpu.make_async_remote_copy(
-            src_ref=ubuf.at[j_me, r], dst_ref=ubuf.at[j_me, r], send_sem=us_sem.at[k, r], recv_sem=ur_sem.at[k, r],
+            src_ref=ubuf.at[j_me, r], dst_ref=ubuf.at[j_me, r], send_sem=us_sem, recv_sem=ur_sem.at[r],
             device_id=(0, peer, side), device_id_type=MESH)
 
     for r in range(CHUNKS):
@@ -351,8 +349,8 @@
 
     wd_own.wait()
     with jax.named_scope("wdwait"):
-        for k in range(1, GRP):
-            wd_copy(k).wait_recv()
+        peers = wd_b.at[pl.ds(0, GRP - 1)]
+        pltpu.make_async_copy(peers, peers, wdr_sem).wait()
 
     per = 64 // CHUNKS
 
@@ -360,8 +358,8 @@
 
     def finish(r):
         with jax.named_scope("uwait"):
-            for k in range(1, GRP):
-                u_copy(k, r).wait_recv()
+            peers = ubuf.at[pl.ds(0, GRP - 1), r]
+            pltpu.make_async_copy(peers, peers, ur_sem.at[r]).wait()
         with jax.named_scope("down"):
             u_all = jnp.concatenate([ubuf[j, r] for j in range(GRP)], axis=1)
             y = jnp.dot(u_all, wd_b[...].reshape(GRP * FFC, NC), preferred_element_type=F32)
@@ -373,7 +371,7 @@
             ax, ay, az = [(a + fx) % 2 for a in range(2)], [(b + cy) % 4 for b in range(4)], [(c + fz) % 2 for c in range(2)]
             px = [jnp.where(a == 0, xs[0], xs[1]) for a in ax]
             for i in range(per):
-                a, b, c, t = i % 2, 3 - (i // 2) % 4, 1 - (i // 8) % 2, i // 16
+                a, b, c, t = i % 2, (2, 1, 3, 0)[(i // 2) % 4], 1 - (i // 8) % 2, i // 16
                 k = 2 * (ax[a] + 2 * ay[b] + 8 * az[c]) + t
                 d = flat(px[a], ay[b], height(px[a], ay[b], az[c]))
 
@@ -421,19 +419,15 @@
             out[:, j * NC:(j + 1) * NC] = (x1[:, j * NC:(j + 1) * NC] + y.astype(BF16).astype(F32)).astype(BF16)
 
     with jax.named_scope("drain"):
-        for k in range(1, GRP):
-            wd_copy(k).wait_send()
-            for r in range(CHUNKS):
-                u_copy(k, r).wait_send()
-        for n in range(6):
-            p_copy(n).wait_send()
-        for q in range(3):
-            @pl.when(source)
-            def _(q=q):
-                some = wkv_b.at[0, pl.ds(0, 15 * 16)]
-                pltpu.make_async_copy(some, some, a1s.at[q]).wait()
-            most = hbuf.at[q, pl.ds(0, 3)]
-            pltpu.make_async_copy(most, most, a2s.at[q]).wait()
+        for ref, sem in ((wd_b.at[pl.ds(0, GRP - 1)], wds_sem), (ubuf.at[pl.ds(0, GRP - 1)], us_sem), (p_own, ps_sem)):
+            pltpu.make_async_copy(ref, ref, sem).wait()
+        @pl.when(source)
+        def _():
+            some = wkv_b.at[0, pl.ds(0, 3 * 15 * 16)]
+            pltpu.make_async_copy(some, some, a1s).wait()
+
+        most = hbuf.at[:, pl.ds(0, 3)]
+        pltpu.make_async_copy(most, most, a2s).wait()
         wait_blocks(ysend, ys_sem)
 
 
@@ -461,9 +455,10 @@
         return pl.pallas_call(
             body,
             out_shape=jax.ShapeDtypeStruct((4, D), BF16),
-            in_specs=[pl.BlockSpec(memory_space=pltpu.SMEM)] + [hbm] * 12,
+            in_specs=[hbm] * 13,
             out_specs=vmem,
             scratch_shapes=[
+                pltpu.SMEM((8,), jnp.int32),
                 pltpu.VMEM((8, D), BF16),
                 pltpu.VMEM((1, D), F32),
                 pltpu.VMEM((6, 1, 512), F32),
@@ -488,9 +483,8 @@
                 pltpu.VMEM((64, 4, NC), F32),
                 pltpu.VMEM((2, 8, 128), F32),
                 pltpu.VMEM((24, 128), jnp.int32),
-                dma((4,)), dma((2,)), dma((2, D // KVC)), dma((2, 2)), dma((6,)), dma((2,)), dma, dma((GRP,)), dma((GRP,)),
-                dma((6,)), dma((6,)), dma((3,)), dma((3, 4)), dma((3,)), dma((3,)),
-                dma((GRP, CHUNKS)), dma((GRP, CHUNKS)), dma, dma,
+                dma((5,)), dma((2,)), dma((2,)), dma((2, 2)), dma((6,)), dma((2,)), dma, dma, dma,
+                dma, dma, dma, dma((3, 4)), dma, dma, dma, dma((CHUNKS,)), dma, dma,
             ],
             compiler_params=pltpu.CompilerParams(
                 collective_id=0, has_side_effects=True, vmem_limit_bytes=60 * 1024 * 1024),

time: 47.4 us -> 46 us (0.970)
  Pallas kernels: 45.8 us -> 44.5 us
    pallas_call x1, Pallas kernels: 45.8 us -> 44.5 us  [device_fn(): pl.pallas_call(body, out_shape=jax.ShapeDtypeStruct((4, D), BF16), in_spe...]
where the time goes in v5:
time: 46 us; the launch traced here: 45.9 us
  Pallas kernels  44.5 us (97%)
  local copies, waits for them, and re-layouts  1.36 us (3%)
    pallas_call x1, Pallas kernels, device_fn(): pl.pallas_call(body, out_shape=jax.ShapeDtypeStruct((4, D), BF16), in_spe...  44.5 us
    unnamed x1, local copies, waits for them, and re-layouts  1.36 us

profile of v5, /device:TPU:1, one launch (start us, length us, event | category | flops | bytes accessed | tf_op | source)
XLA Modules:
  0.0 45.9 jit_solution(4203100592335454349)
XLA Ops:
  0.0 44.5 %decode_layer.1 = bf16[4,3072]{1,0:T(4,128)(2,1)} custom-call(s32[8]{0:T(128)} %lens_h.1, bf16[8,3072]{1,0:T(8,128)(2,1)} %hid_h.1, f32[1,3072]{1,0:T(1,128)} %again_h.1, f32[6,1,512]{2,1,0:T(1,128)} %bitcast.1, f32[1,128]{1,0:T(1,128)} %constant.2.clone.freq_h, bf16[1,8,8,256,128]{4,3,2,1,0:T(8,128)(2,1)} %kc.1, bf16[1,8,8,256,128]{4,3,2,1,0:T(8,128)(2,1)} %vc.1, ...), custom_call_target="tpu_custom_call" | custom-call | tf_op jit(solution)/shard_map/decode_layer/pallas_call | solution.py:455
  44.5 1.4 %copy.15 = bf16[4,3072]{1,0:T(4,128)(2,1)} copy(bf16[4,3072]{1,0:T(4,128)(2,1)} %decode_layer.1) | data formatting | bytes 49152

commit v6 on v5

--- a/solution.py
+++ b/solution.py
@@ -283,26 +283,21 @@
                             ring, row, col = at[q]
                             block = hbuf.at[q, ring, row, col // 2]
                             pltpu.make_async_remote_copy(
-                                src_ref=block, dst_ref=block, send_sem=a1s, recv_sem=a1r.at[q, (4 - i) % 4],
+                                src_ref=block, dst_ref=block, send_sem=a1s, recv_sem=a1r.at[(4 - i) % 4],
                                 device_id=(0, chip_at(q, ring, (row + i) % 4, (col + j) % 4), side),
                                 device_id_type=MESH).start()
 
-    def recv_row(q, sem):
-        some = hbuf.at[q, 0, 0]
-        pltpu.make_async_copy(some, some, sem).wait()
+    def recv_rows(g):
+        def wait(some):
+            pltpu.make_async_copy(some, some, a1r.at[ORDER[g]]).wait()
+
+        if g == 0:
+            pl.when(source)(lambda: wait(hbuf.at[:, 0, 0, 0]))
+            pl.when(jnp.logical_not(source))(lambda: wait(hbuf.at[:, 0, 0]))
+        else:
+            wait(hbuf.at[:, 0, 0])
 
     def own_row(g, q):
-        if g == 0:
-            @pl.when(source)
-            def _():
-                some = hbuf.at[q, 0, 0, 0]
-                pltpu.make_async_copy(some, some, a1r.at[q, 0]).wait()
-
-            @pl.when(jnp.logical_not(source))
-            def _():
-                recv_row(q, a1r.at[q, 0])
-        else:
-            recv_row(q, a1r.at[q, ORDER[g]])
         ring, row, col = at[q]
         part = hbuf.at[q, ring, (row + ORDER[g]) % 4]
         for step in (2, 1, 3):
@@ -312,6 +307,7 @@
 
     for g in range(4):
         with jax.named_scope(f"own_row{g}"):
+            recv_rows(g)
             for q in range(3):
                 own_row(g, q)
     with jax.named_scope("ag2wait"):
@@ -368,20 +364,20 @@
                 ysend[r * per + 2 * i + 1] = y[i * 8 + 4:i * 8 + 8]
         with jax.named_scope("give"):
             xs = half(r)
-            ax, ay, az = [(a + fx) % 2 for a in range(2)], [(b + cy) % 4 for b in range(4)], [(c + fz) % 2 for c in range(2)]
+            ax = [(a + fx) % 2 for a in range(2)]
             px = [jnp.where(a == 0, xs[0], xs[1]) for a in ax]
             for i in range(per):
-                a, b, c, t = i % 2, (2, 1, 3, 0)[(i // 2) % 4], 1 - (i // 8) % 2, i // 16
-                k = 2 * (ax[a] + 2 * ay[b] + 8 * az[c]) + t
-                d = flat(px[a], ay[b], height(px[a], ay[b], az[c]))
+                a, y, h, t = i % 2, (i // 2) % 4, (i // 8) % 2, i // 16
+                k = 2 * (ax[a] + 2 * y + 8 * h) + t
+                d = flat(px[a], y, height(px[a], y, h))
 
                 def start(k=k, d=d, t=t):
                     pltpu.make_async_remote_copy(
                         src_ref=ysend.at[r * per + k], dst_ref=yrecv.at[dev], send_sem=ys_sem, recv_sem=yr_sem,
                         device_id=(0, d, t), device_id_type=MESH).start()
 
-                if r == CHUNKS - 1 and not (a or b or c):
-                    pl.when(jnp.logical_not(jnp.logical_and(source, side == t)))(start)
+                if r == CHUNKS - 1:
+                    pl.when(jnp.logical_or(d != dev, side != t))(start)
                 else:
                     start()
 
@@ -484,7 +480,7 @@
                 pltpu.VMEM((2, 8, 128), F32),
                 pltpu.VMEM((24, 128), jnp.int32),
                 dma((5,)), dma((2,)), dma((2,)), dma((2, 2)), dma((6,)), dma((2,)), dma, dma, dma,
-                dma, dma, dma, dma((3, 4)), dma, dma, dma, dma((CHUNKS,)), dma, dma,
+                dma, dma, dma, dma((4,)), dma, dma, dma, dma((CHUNKS,)), dma, dma,
             ],
             compiler_params=pltpu.CompilerParams(
                 collective_id=0, has_side_effects=True, vmem_limit_bytes=60 * 1024 * 1024),

time: 46 us -> 45.9 us (level)
  no operation moved by 1% of the time
where the time goes in v6:
time: 45.9 us; the launch traced here: 45.7 us
  Pallas kernels  44.3 us (97%)
  local copies, waits for them, and re-layouts  1.36 us (3%)
    pallas_call x1, Pallas kernels, device_fn(): pl.pallas_call(body, out_shape=jax.ShapeDtypeStruct((4, D), BF16), in_spe...  44.3 us
    unnamed x1, local copies, waits for them, and re-layouts  1.36 us

profile of v6, /device:TPU:1, one launch (start us, length us, event | category | flops | bytes accessed | tf_op | source)
XLA Modules:
  0.0 45.7 jit_solution(3488797207179464352)
XLA Ops:
  0.0 44.3 %decode_layer.1 = bf16[4,3072]{1,0:T(4,128)(2,1)} custom-call(s32[8]{0:T(128)} %lens_h.1, bf16[8,3072]{1,0:T(8,128)(2,1)} %hid_h.1, f32[1,3072]{1,0:T(1,128)} %again_h.1, f32[6,1,512]{2,1,0:T(1,128)} %bitcast.1, f32[1,128]{1,0:T(1,128)} %constant.2.clone.freq_h, bf16[1,8,8,256,128]{4,3,2,1,0:T(8,128)(2,1)} %kc.1, bf16[1,8,8,256,128]{4,3,2,1,0:T(8,128)(2,1)} %vc.1, ...), custom_call_target="tpu_custom_call" | custom-call | tf_op jit(solution)/shard_map/decode_layer/pallas_call | solution.py:451
  44.3 1.4 %copy.15 = bf16[4,3072]{1,0:T(4,128)(2,1)} copy(bf16[4,3072]{1,0:T(4,128)(2,1)} %decode_layer.1) | data formatting | bytes 49152
